TPU v7x, 128 devices: a whole 4x4x4 slice. The times are simulated.
128 devices in a mesh: mp: 1, dp: 128 (over z, y, x, core).
Axes of the slice: x: 4, y: 4, z: 4, core: 2. Of those that a mesh axis runs over, the one named last changes fastest.
Arguments:
- grad_partial: float32 [128, 1, 2048, 1024], P(('mp', 'dp'))
- momentum: float32 [1, 2048, 1024], P('mp', 'dp')
- weight: float32 [1, 2048, 1024], P('mp', 'dp')
Outputs:
- output 1: float32 [1, 2048, 1024], P('mp', 'dp')
- output 2: float32 [1, 2048, 1024], P('mp', 'dp')
- output 3: bfloat16 [1, 2048, 1024], P('mp')
All inputs are finite; a program needn't handle non-finite values.
Results may differ from a plain program's by a relative error of at most 0.0159465.
Values are sent between devices in bfloat16 or wider.
A program may use at most 1 GiB of HBM per device.

v0:
```python
import math
import jax
import jax.numpy as jnp
from jax import lax
from jax.sharding import PartitionSpec as P

MOMENTUM = 0.95
LEARN_RATE = 2.0
WEIGHT_DECAY = 0.25
NS_STEPS = 5
COEF_A = 3.4445
COEF_B = -4.7750
COEF_C = 2.0315


def orthogonalise(update):
    num_rows, num_cols = update.shape[1], update.shape[2]
    as_float = update.astype(jnp.float32)
    sq_norm = jnp.sum(as_float * as_float, axis=(1, 2), keepdims=True)
    ortho = (as_float / (jnp.sqrt(sq_norm) + 1e-7)).astype(jnp.bfloat16)
    if num_rows <= num_cols:
        gram_form, apply_form = 'qkl,qjl->qkj', 'qkj,qjl->qkl'
    else:
        gram_form, apply_form = 'qlk,qlj->qkj', 'qkj,qlj->qlk'
    for _ in range(NS_STEPS):
        gram = jnp.einsum(gram_form, ortho, ortho, preferred_element_type=jnp.float32).astype(jnp.bfloat16)
        gram_sq = jnp.einsum('qkj,qji->qki', gram, gram, preferred_element_type=jnp.float32)
        poly = (COEF_B * gram.astype(jnp.float32) + COEF_C * gram_sq).astype(jnp.bfloat16)
        ortho = (COEF_A * ortho.astype(jnp.float32) + jnp.einsum(apply_form, poly, ortho, preferred_element_type=jnp.float32)).astype(jnp.bfloat16)
    return ortho


def solution(mesh):
    group_size = mesh.shape['dp']

    def local_step(grad_part, momentum, weight):
        grad = lax.psum_scatter(grad_part[0], 'dp', scatter_dimension=1, tiled=True) / group_size
        new_momentum = MOMENTUM * momentum + grad
        direction = (grad + MOMENTUM * new_momentum).astype(jnp.bfloat16)
        num_mats, slab_rows, num_cols = direction.shape
        num_rows = group_size * slab_rows
        num_rounds = -(-num_mats // group_size)
        padded = jnp.pad(direction, ((0, num_rounds * group_size - num_mats), (0, 0), (0, 0)))
        per_round = padded.reshape(num_rounds, group_size, slab_rows, num_cols)
        gathered = lax.all_to_all(per_round, 'dp', 1, 2, tiled=True)
        ortho_full = orthogonalise(gathered.reshape(num_rounds, num_rows, num_cols))
        returned = lax.all_to_all(ortho_full.reshape(num_rounds, 1, num_rows, num_cols), 'dp', 2, 1, tiled=True)
        ortho_slab = returned.reshape(num_rounds * group_size, slab_rows, num_cols)[:num_mats]
        scale = 0.2 * math.sqrt(max(num_rows, num_cols))
        new_weight = weight - LEARN_RATE * (scale * ortho_slab.astype(jnp.float32) + WEIGHT_DECAY * weight)
        weight_bf16 = lax.all_gather(new_weight.astype(jnp.bfloat16), 'dp', axis=1, tiled=True)
        return new_momentum, new_weight, weight_bf16

    return jax.shard_map(local_step, mesh=mesh, in_specs=(P(('mp', 'dp')), P('mp', 'dp'), P('mp', 'dp')), out_specs=(P('mp', 'dp'), P('mp', 'dp'), P('mp')), check_vma=False)
```

profile of v0, /device:TPU:1, one launch (start us, length us, event | category | flops | bytes accessed | tf_op | source)
XLA Modules:
  0.0 573.5 jit_solution(16917497493403632820)
XLA Ops:
  7.2 0.0 all-reduce.4.cloned.1.call-start
  7.2 8.1 %squeeze.3 = f32[1,2048,1024]{2,0,1:T(1,128)} reshape(f32[1,1,2048,1024]{3,2,1,0:T(8,128)} %param.3) | data formatting | bytes 16777216 | tf_op jit(solution)/shard_map/squeeze | solution.py:37
  15.3 0.0 copy-start.2
  15.3 0.0 all-reduce.4.cloned.1.call-update
  15.3 0.0 all-gather.2.cloned.1.call-start
  15.4 0.8 copy-done.2
  16.2 163.9 %all-reduce.4.cloned.1.call-done = f32[1,2048,1024]{2,0,1:T(1,128)} async-done(((f32[1,2048,1024]{2,0,1:T(1,128)}), f32[1,2048,1024]{2,0,1:T(1,128)}) %all-reduce.4.cloned.1.call-update) | async-done | bytes 8388624
  180.1 1.0 add_convert_fusion.10
  181.1 0.5 pad_bitcast_fusion
  181.6 2.3 copy.25
  184.0 67.6 %all_to_all.21 = bf16[1,128,16,1024]{3,2,0,1:T(8,128)(2,1)S(1)} all-to-all(bf16[1,128,16,1024]{3,2,0,1:T(8,128)(2,1)S(1)} %copy.25), channel_id=1, replica_groups=mesh['mp'=1,'dp'=128] {'dp'}, dimensions={1} | all-to-all | bytes 8388608 | tf_op jit(solution)/shard_map/all_to_all | solution.py:45
  251.6 0.0 copy-start
  251.6 2.0 copy-done
  253.6 2.8 fusion
  257.1 4.7 fusion.1
  261.7 4.3 copy.27
  266.1 4.8 fusion.3
  270.8 12.3 %add_convert_fusion.4 = bf16[2048,1024]{1,0:T(8,128)(2,1)} fusion(bf16[2048,1024]{1,0:T(8,128)(2,1)} %bitcast.61, bf16[1024,1024,1]{1,0,2:T(8,128)(2,1)S(1)} %fusion.3), kind=kOutput, calls=%fused_computation.8 | convolution fusion | flops 6456082432 | bytes 10485760 | tf_op jit(solution)/shard_map/qkj,qlj->qlk/dot_general | solution.py:29
  283.1 8.0 %fusion.13 = bf16[1024,1024]{1,0:T(8,128)(2,1)S(1)} fusion(bf16[2048,1024]{1,0:T(8,128)(2,1)} %add_convert_fusion.4), kind=kOutput, calls=%fused_computation.32 | convolution fusion | flops 4294967296 | bytes 6291456 | tf_op jit(solution)/shard_map/qlk,qlj->qkj/dot_general | solution.py:26
  291.2 11.8 %add_convert_fusion.3 = bf16[2048,1024]{1,0:T(8,128)(2,1)} fusion(bf16[2048,1024]{1,0:T(8,128)(2,1)} %add_convert_fusion.4, bf16[1024,1024]{1,0:T(8,128)(2,1)S(1)} %fusion.13), kind=kOutput, calls=%fused_computation.7 | convolution fusion | flops 6456082432 | bytes 10485760 | tf_op jit(solution)/shard_map/qkj,qlj->qlk/dot_general | solution.py:29
  303.0 8.0 %fusion.14 = bf16[1024,1024]{1,0:T(8,128)(2,1)S(1)} fusion(bf16[2048,1024]{1,0:T(8,128)(2,1)} %add_convert_fusion.3), kind=kOutput, calls=%fused_computation.33 | convolution fusion | flops 4294967296 | bytes 6291456 | tf_op jit(solution)/shard_map/qlk,qlj->qkj/dot_general | solution.py:26
  311.0 11.8 %add_convert_fusion.2 = bf16[2048,1024]{1,0:T(8,128)(2,1)} fusion(bf16[2048,1024]{1,0:T(8,128)(2,1)} %add_convert_fusion.3, bf16[1024,1024]{1,0:T(8,128)(2,1)S(1)} %fusion.14), kind=kOutput, calls=%fused_computation.6 | convolution fusion | flops 6456082432 | bytes 10485760 | tf_op jit(solution)/shard_map/qkj,qlj->qlk/dot_general | solution.py:29
  322.8 8.0 %fusion.15 = bf16[1024,1024]{1,0:T(8,128)(2,1)S(1)} fusion(bf16[2048,1024]{1,0:T(8,128)(2,1)} %add_convert_fusion.2), kind=kOutput, calls=%fused_computation.34 | convolution fusion | flops 4294967296 | bytes 6291456 | tf_op jit(solution)/shard_map/qlk,qlj->qkj/dot_general | solution.py:26
  330.9 11.9 %add_convert_fusion.1 = bf16[2048,1024]{1,0:T(8,128)(2,1)} fusion(bf16[2048,1024]{1,0:T(8,128)(2,1)} %add_convert_fusion.2, bf16[1024,1024]{1,0:T(8,128)(2,1)S(1)} %fusion.15), kind=kOutput, calls=%fused_computation.5 | convolution fusion | flops 6456082432 | bytes 10485760 | tf_op jit(solution)/shard_map/qkj,qlj->qlk/dot_general | solution.py:29
  342.7 8.0 %fusion.16 = bf16[1024,1024]{1,0:T(8,128)(2,1)S(1)} fusion(bf16[2048,1024]{1,0:T(8,128)(2,1)} %add_convert_fusion.1), kind=kOutput, calls=%fused_computation.35 | convolution fusion | flops 4294967296 | bytes 6291456 | tf_op jit(solution)/shard_map/qlk,qlj->qkj/dot_general | solution.py:26
  350.8 11.7 %fusion.2 = bf16[1,1,2048,1024]{3,2,1,0:T(8,128)(2,1)} fusion(bf16[2048,1024]{1,0:T(8,128)(2,1)} %add_convert_fusion.1, bf16[1024,1024]{1,0:T(8,128)(2,1)S(1)} %fusion.16), kind=kOutput, calls=%fused_computation.9 | convolution fusion | flops 6456082432 | bytes 10485760 | tf_op jit(solution)/shard_map/qkj,qlj->qlk/dot_general | solution.py:29
  362.5 8.6 %copy.38 = bf16[1,1,2048,1024]{3,1,0,2:T(2,128)(2,1)} copy(bf16[1,1,2048,1024]{3,2,1,0:T(8,128)(2,1)} %fusion.2) | data formatting | bytes 8388608 | tf_op jit(solution)/shard_map/reshape | solution.py:47
  371.1 0.5 broadcast.101
  371.6 26.3 %reduce.3 = bf16[2048,1024]{1,0:T(8,128)(2,1)} reduce(bf16[2048,1,1,1024]{3,2,1,0:T(2,128)(2,1)} %bitcast.58, bf16[]{:T(256)} %broadcast.101), dimensions={1,2}, to_apply=%bitcast.57.reduce_sub_computation | reduce | bytes 8388610
  397.9 7.8 %reshape.205 = bf16[128,2,8192]{2,1,0:T(2,128)(2,1)} reshape(bf16[2048,1024]{1,0:T(8,128)(2,1)} %reduce.3) | data formatting | bytes 8388608
  405.7 65.5 %all_to_all.22 = bf16[128,2,8192]{2,1,0:T(2,128)(2,1)} all-to-all(bf16[128,2,8192]{2,1,0:T(2,128)(2,1)} %reshape.205), channel_id=1, replica_groups=mesh['mp'=1,'dp'=128] {'dp'}, dimensions={0} | all-to-all | bytes 8388608 | tf_op jit(solution)/shard_map/all_to_all | solution.py:47
  471.2 19.8 %reshape.206 = bf16[2048,1,1,1024]{3,2,1,0:T(2,128)(2,1)} reshape(bf16[128,2,8192]{2,1,0:T(2,128)(2,1)} %all_to_all.22) | data formatting | bytes 8388608
  491.0 0.0 copy-start.1
  491.0 5.1 copy.32
  496.1 0.0 copy-done.1
  496.1 0.7 fusion.11
  496.7 0.0 all-gather.2.cloned.1.call-update
  496.8 0.6 copy.30
  497.4 64.4 %all-gather.2.cloned.1.call-done = bf16[1,2048,1024]{2,1,0:T(8,128)(2,1)} async-done(((bf16[1,16,1024]{2,1,0:T(8,128)(2,1)}), bf16[1,2048,1024]{2,1,0:T(8,128)(2,1)}) %all-gather.2.cloned.1.call-update) | async-done | bytes 4194320 | tf_op jit(solution)/shard_map/all_gather | solution.py:51
  561.8 4.6 copy.41
  (1 shorter events, 0.0 us)
Async XLA Ops:
  7.2 172.9 %all-reduce.4.cloned.1.call-start = ((), (), s32[]{:S(2)}) async-start(), calls=%async_computation.3 | async-start | bytes 16777216
  15.3 0.8 copy-start.2
  15.3 546.5 %all-gather.2.cloned.1.call-start = ((), (), s32[]{:S(2)}) async-start(), calls=%async_computation.2 | async-start | bytes 4227072 | tf_op jit(solution)/shard_map/all_gather | solution.py:51
  251.6 2.0 copy-start
  491.0 5.1 copy-start.1
Sparse Core Ops, SparseCore 0:
  15.4 164.6 all-reduce.3
  496.9 64.8 all-gather.1
where the time goes:
time: 578 us; the launch traced here: 574 us
  waiting for transfers between devices  228 us (39%)
  blocking collectives  133 us (23%)
  matrix products  96.4 us (17%)
  local copies, waits for them, and re-layouts  65.2 us (11%)
  other arithmetic  35.3 us (6%)
  between operations  15.1 us (3%)
    unnamed x3, waiting for transfers between devices  164 us
    all_to_all x1, blocking collectives, local_step(): gathered = lax.all_to_all(per_round, 'dp', 1, 2, tiled=True)  67.6 us
    all_to_all x1, blocking collectives, local_step(): lax.all_to_all(ortho_full.reshape(num_rounds, 1, num_rows, num_cols), 'dp...  65.5 us
    all_gather x1, waiting for transfers between devices, local_step(): lax.all_gather(new_weight.astype(jnp.bfloat16), 'dp', axis=1, tiled=True)  64.4 us
    dot_general x5, matrix products, orthogonalise(): jnp.einsum(apply_form, poly, ortho, preferred_element_type=jnp.float32)  59.4 us
    unnamed x12, local copies, waits for them, and re-layouts  41.2 us
    dot_general x5, matrix products, orthogonalise(): jnp.einsum(gram_form, ortho, ortho, preferred_element_type=jnp.float32)  36.9 us
    unnamed x1, other arithmetic  26.3 us
  transfers between devices with their start and end apart: 2, of which 2 were waited for; matrix products, arithmetic and copies ran while one was open for 0% of the time, Pallas kernels for 0%

commit v1 on v0

v1 whole, which is shorter than its diff:
```python
import math
import jax
import jax.numpy as jnp
from jax import lax
from jax.experimental import pallas as pl
from jax.experimental.pallas import tpu as pltpu
from jax.sharding import PartitionSpec as P

MOMENTUM = 0.95
LEARN_RATE = 2.0
WEIGHT_DECAY = 0.25
NS_STEPS = 5
COEF_A = 3.4445
COEF_B = -4.7750
COEF_C = 2.0315

MESH = pl.DeviceIdType.MESH
RING = 4
CHIPS = 64
GROUP = 128
SLAB = 16
COLS = 1024
ROWS = 2048
Z, Y, X = 0, 1, 2
PARTS = ((0, 384, (X, Y, Z)), (384, 384, (Y, Z, X)), (768, 256, (Z, X, Y)))


class Place:
    def __init__(self):
        me = lax.axis_index('dp')
        self.core = lax.rem(me, 2)
        chip = lax.div(me, 2)
        self.xyz = (lax.div(chip, 16), lax.rem(lax.div(chip, 4), 4), lax.rem(chip, 4))

    def index(self, xyz, core):
        return ((xyz[0] * RING + xyz[1]) * RING + xyz[2]) * 2 + core

    def shifted(self, axis, by):
        return lax.rem(self.xyz[axis] + (by % RING), RING)

    def neighbour(self, axis, by):
        xyz = list(self.xyz)
        xyz[axis] = self.shifted(axis, by)
        return {'dp': self.index(xyz, self.core)}

    def partner(self):
        return {'dp': self.index(self.xyz, 1 - self.core)}


def greet(place):
    barrier = pltpu.get_barrier_semaphore()
    peers = [place.partner()] + [place.neighbour(a, s) for a in (Z, Y, X) for s in (1, -1, 2)]
    for peer in peers:
        pl.semaphore_signal(barrier, inc=1, device_id=peer, device_id_type=MESH)
    pl.semaphore_wait(barrier, len(peers))


def at(fixed, rows, cols):
    return tuple(fixed.get(a, slice(None)) for a in (Z, Y, X)) + (rows, cols)


def send(src, dst, ssem, rsem, peer):
    copy = pltpu.make_async_remote_copy(src_ref=src, dst_ref=dst, send_sem=ssem, recv_sem=rsem, device_id=peer, device_id_type=MESH)
    copy.start()
    return copy


ALL = slice(None)
LOW, HIGH = pl.ds(0, 8), pl.ds(8, 8)


def reduce_phase(place, acc, ring_refs, ssem, rsem, part, phase, ready):
    first, width, order = PARTS[part]
    axis = order[phase]
    cols = pl.ds(first, width)
    near_l, near_r, far_l, far_r = ring_refs
    fixed = {a: place.xyz[a] for a in order[:phase]}
    right, left = place.neighbour(axis, 1), place.neighbour(axis, -1)

    def chunk(by, rows):
        return at({**fixed, axis: place.shifted(axis, by)}, rows, cols)

    def sub(rows):
        return tuple(ALL for _ in range(2 - phase)) + (rows, cols)

    started = []
    sems = lambda i: (ssem.at[part, phase, i], rsem.at[part, phase, i])
    ready(2)
    started.append(send(acc.at[chunk(2, LOW)], far_l.at[sub(ALL)], *sems(0), right))
    started.append(send(acc.at[chunk(2, HIGH)], far_r.at[sub(ALL)], *sems(1), left))
    yield
    ready(1)
    started.append(send(acc.at[chunk(1, HIGH)], near_l.at[sub(HIGH)], *sems(2), right))
    yield
    ready(-1)
    started.append(send(acc.at[chunk(-1, LOW)], near_r.at[sub(LOW)], *sems(3), left))
    yield
    started[0].wait_recv()
    acc[chunk(1, LOW)] += far_l[sub(ALL)]
    started.append(send(acc.at[chunk(1, LOW)], near_l.at[sub(LOW)], *sems(4), right))
    yield
    started[1].wait_recv()
    acc[chunk(-1, HIGH)] += far_r[sub(ALL)]
    started.append(send(acc.at[chunk(-1, HIGH)], near_r.at[sub(HIGH)], *sems(5), left))
    yield
    ready(0)
    yield
    for i in (2, 3, 4, 5):
        started[i].wait_recv()
    acc[chunk(0, ALL)] += near_l[sub(ALL)] + near_r[sub(ALL)]
    return started


def gather_phase(place, buf, ssem, rsem, part, phase, on_piece):
    first, width, order = PARTS[part]
    axis = order[phase]
    cols = pl.ds(first, width)
    fixed = {a: place.xyz[a] for a in order[:phase]}
    right, left, across = place.neighbour(axis, 1), place.neighbour(axis, -1), place.neighbour(axis, 2)
    free = [a for a in (Z, Y, X) if a in order[phase + 1:]]
    sems = lambda i: (ssem.at[part, phase, i], rsem.at[part, phase, i])

    def chunk(by, half=None):
        where = {**fixed, axis: place.shifted(axis, by)}
        if half is not None:
            where[free[0]] = pl.ds(2 * half, 2)
        return at(where, ALL, cols)

    def recv(i, by, half=None):
        there = buf.at[chunk(by, half)]
        pltpu.make_async_remote_copy(src_ref=there, dst_ref=there, send_sem=ssem.at[part, phase, i], recv_sem=rsem.at[part, phase, i], device_id=right, device_id_type=MESH).wait_recv()

    started = []
    mine = buf.at[chunk(0)]
    started.append(send(mine, mine, *sems(0), right))
    started.append(send(mine, mine, *sems(1), left))
    if not free:
        started.append(send(mine, mine, *sems(2), across))
        on_piece(0, chunk(0))
        yield
        recv(0, -1)
        recv(1, 1)
        recv(2, 2)
    else:
        on_piece(0, chunk(0))
        yield
        recv(0, -1)
        there = buf.at[chunk(-1, 0)]
        started.append(send(there, there, *sems(2), right))
        on_piece(1, chunk(-1))
        yield
        recv(1, 1)
        there = buf.at[chunk(1, 1)]
        started.append(send(there, there, *sems(3), left))
        on_piece(2, chunk(1))
        yield
        recv(2, 2, 0)
        on_piece(3, chunk(2, 0))
        yield
        recv(3, 2, 1)
        on_piece(4, chunk(2, 1))
    return started


def run_together(generators):
    started, live = [], list(generators)
    while live:
        left = []
        for g in live:
            try:
                next(g)
                left.append(g)
            except StopIteration as stop:
                started.extend(stop.value)
        live = left
    return started


def comm_kernel(grad, momentum, new_momentum, mine, other, acc, half, *scratch):
    ring = scratch[:12]
    load_sem, pair_ssem, pair_rsem, rs_ssem, rs_rsem, ag_ssem, ag_rsem, fw_ssem, fw_rsem = scratch[12:]
    place = Place()
    stages = (2, 1, -1, 0)
    loads, swaps = {}, {}
    for s, by in enumerate(stages):
        for p, (first, width, order) in enumerate(PARTS):
            axis = order[0]
            block = {axis: place.shifted(axis, by)}
            z, y, x, r, c = at(block, ALL, pl.ds(first, width))
            loads[p, by] = pltpu.make_async_copy(grad.at[z, y, x, place.core, r, c], acc.at[z, y, x, r, c], load_sem.at[p, s])
            loads[p, by].start()
    greet(place)
    for s, by in enumerate(stages):
        for p, (first, width, order) in enumerate(PARTS):
            axis = order[0]
            block = {axis: place.shifted(axis, by)}
            z, y, x, r, c = at(block, ALL, pl.ds(first, width))
            swaps[p, by] = send(grad.at[z, y, x, 1 - place.core, r, c], half.at[z, y, x, r, c], pair_ssem.at[p, s], pair_rsem.at[p, s], place.partner())

    def ready(part):
        def chunk_ready(by):
            first, width, order = PARTS[part]
            here = at({order[0]: place.shifted(order[0], by)}, ALL, pl.ds(first, width))
            loads[part, by].wait()
            swaps[part, by].wait_recv()
            acc[here] += half[here]
        return chunk_ready

    sent = list(swaps.values())
    for phase in range(3):
        sent += run_together([reduce_phase(place, acc, ring[4 * phase:4 * phase + 4], rs_ssem, rs_rsem, p, phase, ready(p) if phase == 0 else (lambda by: None)) for p in range(3)])

    z, y, x = place.xyz
    g = acc[z, y, x] / GROUP
    mom = MOMENTUM * momentum[...] + g
    new_momentum[...] = mom
    mine[z, y, x] = (g + MOMENTUM * mom).astype(jnp.bfloat16)

    forwards = []

    def forward(part):
        def on_piece(i, where):
            forwards.append(send(mine.at[where], other.at[where], fw_ssem.at[part, i], fw_rsem.at[part, i], place.partner()))
        return on_piece

    for phase in (2, 1, 0):
        sent += run_together([gather_phase(place, mine, ag_ssem, ag_rsem, p, phase, forward(p) if phase == 0 else (lambda i, w: None)) for p in range(3)])
    for copy in forwards:
        copy.wait_recv()
    for copy in sent + forwards:
        copy.wait_send()


def comm(grad, momentum):
    ring = []
    for lead in ((RING, RING), (RING,), ()):
        ring += [pltpu.VMEM(lead + (SLAB, COLS), jnp.float32)] * 2 + [pltpu.VMEM(lead + (8, COLS), jnp.float32)] * 2
    dma = pltpu.SemaphoreType.DMA
    cube = (RING, RING, RING, SLAB, COLS)
    vmem = pl.BlockSpec(memory_space=pltpu.VMEM)
    return pl.pallas_call(
        comm_kernel,
        out_shape=(jax.ShapeDtypeStruct((SLAB, COLS), jnp.float32), jax.ShapeDtypeStruct(cube, jnp.bfloat16), jax.ShapeDtypeStruct(cube, jnp.bfloat16)),
        in_specs=[pl.BlockSpec(memory_space=pl.ANY), vmem],
        out_specs=(vmem, vmem, vmem),
        scratch_shapes=[pltpu.VMEM(cube, jnp.float32), pltpu.VMEM(cube, jnp.float32), *ring,
                        dma((3, 4)), dma((3, 4)), dma((3, 4)), dma((3, 3, 6)), dma((3, 3, 6)), dma((3, 3, 4)), dma((3, 3, 4)), dma((3, 5)), dma((3, 5))],
        compiler_params=pltpu.CompilerParams(collective_id=0, has_side_effects=True, vmem_limit_bytes=60 << 20),
        name='reduce_gather',
    )(grad, momentum)


def orthogonalise(update):
    as_float = update.astype(jnp.float32)
    sq_norm = jnp.sum(as_float * as_float)
    ortho = (as_float / (jnp.sqrt(sq_norm) + 1e-7)).astype(jnp.bfloat16)
    for _ in range(NS_STEPS):
        gram = jnp.einsum('lk,lj->kj', ortho, ortho, preferred_element_type=jnp.float32).astype(jnp.bfloat16)
        gram_sq = jnp.einsum('kj,ji->ki', gram, gram, preferred_element_type=jnp.float32)
        poly = (COEF_B * gram.astype(jnp.float32) + COEF_C * gram_sq).astype(jnp.bfloat16)
        ortho = (COEF_A * ortho.astype(jnp.float32) + jnp.einsum('kj,lj->lk', poly, ortho, preferred_element_type=jnp.float32)).astype(jnp.bfloat16)
    return ortho


def solution(mesh):
    def local_step(grad_part, momentum, weight):
        grad = grad_part.reshape(RING, RING, RING, 2, SLAB, COLS)
        new_momentum, mine, other = comm(grad, momentum[0])
        core = lax.rem(lax.axis_index('dp'), 2)
        first = core == 0
        pair = jnp.stack([jnp.where(first, mine, other), jnp.where(first, other, mine)], axis=3)
        ortho = orthogonalise(pair.reshape(ROWS, COLS))
        slab = lax.dynamic_slice(ortho, (lax.axis_index('dp') * SLAB, 0), (SLAB, COLS))
        scale = 0.2 * math.sqrt(ROWS)
        new_weight = weight - LEARN_RATE * (scale * slab.astype(jnp.float32)[None] + WEIGHT_DECAY * weight)
        weight_bf16 = lax.all_gather(new_weight.astype(jnp.bfloat16), 'dp', axis=1, tiled=True)
        return new_momentum[None], new_weight, weight_bf16

    return jax.shard_map(local_step, mesh=mesh, in_specs=(P(('mp', 'dp')), P('mp', 'dp'), P('mp', 'dp')), out_specs=(P('mp', 'dp'), P('mp', 'dp'), P('mp')), check_vma=False)
```

time: 578 us -> 263 us (0.46)
  waiting for transfers between devices: 228 us -> 63.5 us
  blocking collectives: 133 us -> 0 us
  Pallas kernels: 0 us -> 66.6 us
  local copies, waits for them, and re-layouts: 65.2 us -> 9.05 us
  other arithmetic: 35.3 us -> 9.55 us
    unnamed x3 -> x1, waiting for transfers between devices: 164 us -> 0.02 us
    all_to_all x2 -> x0, blocking collectives: 133 us -> none  [the longest x1 67.6 us: local_step(): gathered = lax.all_to_all(per_round, 'dp', 1, 2, tiled=True)]
    pallas_call x0 -> x1, Pallas kernels: none -> 66.6 us  [comm(): pl.pallas_call(comm_kernel, out_shape=(jax.ShapeDtypeStruct((SLAB, COLS),...]
    unnamed x12 -> x8, local copies, waits for them, and re-layouts: 41.2 us -> 6.59 us
    unnamed x1 -> x0, other arithmetic: 26.3 us -> none
    reshape x3 -> x0, local copies, waits for them, and re-layouts: 11.5 us -> none  [the longest x1 8.63 us: local_step(): ortho_full.reshape(num_rounds, 1, num_rows, num_cols)]
    squeeze x1 -> x0, local copies, waits for them, and re-layouts: 8.09 us -> none  [local_step(): grad_part[0]]
  transfers between devices with their start and end apart: 2 -> 1, of which waited for: 2 -> 1; matrix products, arithmetic and copies ran while one was open for 0% -> 0% of each run, Pallas kernels for 0% -> 0%
where the time goes in v1:
time: 263 us; the launch traced here: 261 us
  matrix products  96.7 us (37%)
  Pallas kernels  66.6 us (25%)
  waiting for transfers between devices  63.5 us (24%)
  between operations  15.1 us (6%)
  other arithmetic  9.55 us (4%)
  local copies, waits for them, and re-layouts  9.05 us (3%)
    pallas_call x1, Pallas kernels, comm(): pl.pallas_call(comm_kernel, out_shape=(jax.ShapeDtypeStruct((SLAB, COLS),...  66.6 us
    all_gather x1, waiting for transfers between devices, local_step(): lax.all_gather(new_weight.astype(jnp.bfloat16), 'dp', axis=1, tiled=True)  63.5 us
    dot_general x5, matrix products, orthogonalise(): jnp.einsum('kj,lj->lk', poly, ortho, preferred_element_type=jnp.float32)  59.8 us
    dot_general x5, matrix products, orthogonalise(): jnp.einsum('lk,lj->kj', ortho, ortho, preferred_element_type=jnp.float32)  37 us
    unnamed x8, local copies, waits for them, and re-layouts  6.59 us
  transfers between devices with their start and end apart: 1, of which 1 were waited for; matrix products, arithmetic and copies ran while one was open for 0% of the time, Pallas kernels for 0%

profile of v1, /device:TPU:1, one launch (start us, length us, event | category | flops | bytes accessed | tf_op | source)
XLA Modules:
  0.0 260.6 jit_solution(5495889361914610794)
XLA Ops:
  7.2 0.0 all-gather.2.cloned.1.call-start
  7.2 66.6 %reduce_gather.1 = (f32[16,1024]{1,0:T(8,128)}, bf16[4,4,4,16,1024]{4,3,2,1,0:T(8,128)(2,1)}, bf16[4,4,4,16,1024]{4,3,2,1,0:T(8,128)(2,1)}) custom-call(f32[4,4,4,2,16,1024]{5,4,3,2,1,0:T(8,128)} %bitcast.42, f32[16,1024]{1,0:T(8,128)} %bitcast.44), custom_call_target="tpu_custom_call" | custom-call | tf_op jit(solution)/shard_map/reduce_gather/pallas_call | solution.py:241
  73.8 2.5 select_bitcast_fusion.1
  76.3 0.0 copy-start
  76.3 1.3 copy-done
  77.6 3.3 %fusion = f32[]{:T(128)} fusion(bf16[4,4,4,1,16,1024]{5,4,2,1,0,3:T(8,128)(2,1)S(1)} %get-tuple-element.12, bf16[4,4,4,1,16,1024]{5,4,2,1,0,3:T(8,128)(2,1)S(1)} %get-tuple-element.11), kind=kLoop, calls=%fused_computation.2 | loop fusion | flops 8388607 | bytes 4194308 | tf_op jit(solution)/shard_map/reduce_sum | solution.py:255
  81.6 2.3 fusion.1
  83.9 4.8 %bitcast_convert_fusion = bf16[1024,1024]{1,0:T(8,128)(2,1)S(1)} fusion(bf16[4,4,4,2,16,1024]{5,4,2,1,0,3:T(8,128)(2,1)S(1)} %fusion.1), kind=kOutput, calls=%fused_computation.9 | convolution fusion | flops 4296015872 | bytes 6291456 | tf_op jit(solution)/shard_map/lk,lj->kj/dot_general | solution.py:258
  88.7 2.5 copy.8
  91.1 11.7 %add_convert_fusion.3 = bf16[2048,1024]{1,0:T(8,128)(2,1)} fusion(bf16[2048,1024]{1,0:T(8,128)(2,1)} %bitcast.43, bf16[1024,1024]{1,0:T(8,128)(2,1)S(1)} %bitcast_convert_fusion), kind=kOutput, calls=%fused_computation.7 | convolution fusion | flops 6456082432 | bytes 10485760 | tf_op jit(solution)/shard_map/kj,lj->lk/dot_general | solution.py:261
  102.9 8.0 %fusion.19 = bf16[1024,1024]{1,0:T(8,128)(2,1)S(1)} fusion(bf16[2048,1024]{1,0:T(8,128)(2,1)} %add_convert_fusion.3), kind=kOutput, calls=%fused_computation.33 | convolution fusion | flops 4294967296 | bytes 6291456 | tf_op jit(solution)/shard_map/lk,lj->kj/dot_general | solution.py:258
  110.9 11.8 %add_convert_fusion.2 = bf16[2048,1024]{1,0:T(8,128)(2,1)} fusion(bf16[2048,1024]{1,0:T(8,128)(2,1)} %add_convert_fusion.3, bf16[1024,1024]{1,0:T(8,128)(2,1)S(1)} %fusion.19), kind=kOutput, calls=%fused_computation.6 | convolution fusion | flops 6456082432 | bytes 10485760 | tf_op jit(solution)/shard_map/kj,lj->lk/dot_general | solution.py:261
  122.8 8.0 %fusion.20 = bf16[1024,1024]{1,0:T(8,128)(2,1)S(1)} fusion(bf16[2048,1024]{1,0:T(8,128)(2,1)} %add_convert_fusion.2), kind=kOutput, calls=%fused_computation.34 | convolution fusion | flops 4294967296 | bytes 6291456 | tf_op jit(solution)/shard_map/lk,lj->kj/dot_general | solution.py:258
  130.8 12.0 %add_convert_fusion.1 = bf16[2048,1024]{1,0:T(8,128)(2,1)} fusion(bf16[2048,1024]{1,0:T(8,128)(2,1)} %add_convert_fusion.2, bf16[1024,1024]{1,0:T(8,128)(2,1)S(1)} %fusion.20), kind=kOutput, calls=%fused_computation.5 | convolution fusion | flops 6456082432 | bytes 10485760 | tf_op jit(solution)/shard_map/kj,lj->lk/dot_general | solution.py:261
  142.8 8.0 %fusion.21 = bf16[1024,1024]{1,0:T(8,128)(2,1)S(1)} fusion(bf16[2048,1024]{1,0:T(8,128)(2,1)} %add_convert_fusion.1), kind=kOutput, calls=%fused_computation.35 | convolution fusion | flops 4294967296 | bytes 6291456 | tf_op jit(solution)/shard_map/lk,lj->kj/dot_general | solution.py:258
  150.8 11.9 %add_convert_fusion = bf16[2048,1024]{1,0:T(8,128)(2,1)} fusion(bf16[2048,1024]{1,0:T(8,128)(2,1)} %add_convert_fusion.1, bf16[1024,1024]{1,0:T(8,128)(2,1)S(1)} %fusion.21), kind=kOutput, calls=%fused_computation.4 | convolution fusion | flops 6456082432 | bytes 10485760 | tf_op jit(solution)/shard_map/kj,lj->lk/dot_general | solution.py:261
  162.7 8.0 %fusion.22 = bf16[1024,1024]{1,0:T(8,128)(2,1)S(1)} fusion(bf16[2048,1024]{1,0:T(8,128)(2,1)} %add_convert_fusion), kind=kOutput, calls=%fused_computation.36 | convolution fusion | flops 4294967296 | bytes 6291456 | tf_op jit(solution)/shard_map/lk,lj->kj/dot_general | solution.py:258
  170.8 0.0 copy-start.2
  170.8 0.0 copy-start.1
  170.8 12.3 %fusion.7 = f32[2048,1024]{1,0:T(8,128)} fusion(bf16[2048,1024]{1,0:T(8,128)(2,1)} %add_convert_fusion, bf16[1024,1024]{1,0:T(8,128)(2,1)S(1)} %fusion.22), kind=kOutput, calls=%fused_computation.21 | convolution fusion | flops 6447693824 | bytes 14680064 | tf_op jit(solution)/shard_map/kj,lj->lk/dot_general | solution.py:261
  183.1 0.0 copy-done.2
  183.1 1.5 fusion.17
  184.6 0.0 all-gather.2.cloned.1.call-update
  184.7 63.5 %all-gather.2.cloned.1.call-done = bf16[1,2048,1024]{2,1,0:T(8,128)(2,1)} async-done(((bf16[1,16,1024]{2,1,0:T(8,128)(2,1)}), bf16[1,2048,1024]{2,1,0:T(8,128)(2,1)}) %all-gather.2.cloned.1.call-update) | async-done | bytes 4194320 | tf_op jit(solution)/shard_map/all_gather | solution.py:276
  248.2 0.0 copy-done.1
  248.2 0.6 copy.16
  248.8 4.6 %copy.17 = bf16[1,2048,1024]{2,1,0:T(8,128)(2,1)} copy(bf16[1,2048,1024]{2,1,0:T(8,128)(2,1)} %all-gather.2.cloned.1.call-done) | data formatting | bytes 8388608
Async XLA Ops:
  7.2 241.0 %all-gather.2.cloned.1.call-start = ((), (), s32[]{:S(2)}) async-start(), calls=%async_computation | async-start | bytes 4227072 | tf_op jit(solution)/shard_map/all_gather | solution.py:276
  76.3 1.3 copy-start
  170.8 12.4 %copy-start.2 = (f32[1,16,1024]{2,1,0:T(8,128)S(1)}, f32[1,16,1024]{2,1,0:T(8,128)}, u32[]{:S(2)}) copy-start(f32[1,16,1024]{2,1,0:T(8,128)} %param.5) | copy-start | bytes 196612
  170.8 77.4 %copy-start.1 = (f32[16,1024]{1,0:T(8,128)S(1)}, f32[16,1024]{1,0:T(8,128)}, u32[]{:S(2)}) copy-start(f32[16,1024]{1,0:T(8,128)} %get-tuple-element.6) | copy-start | bytes 196612
Sparse Core Ops, SparseCore 0:
  184.8 63.3 all-gather.1

commit v2 on v1

--- a/solution.py
+++ b/solution.py
@@ -176,26 +176,80 @@
     return started
 
 
-def comm_kernel(grad, momentum, new_momentum, mine, other, acc, half, *scratch):
+NT = (((1,), (1,)), ((), ()))
+BLK = 256
+NBLK = COLS // BLK
+
+
+def dot(a, b):
+    return jnp.dot(a, b, preferred_element_type=jnp.float32)
+
+
+def weight_step(place, weight, full, ssem, rsem, step):
+    def piece(part, phase, i):
+        first, width, order = PARTS[part]
+        axis = order[phase]
+        cols = pl.ds(first, width)
+        fixed = {a: place.xyz[a] for a in order[:phase]}
+        free = [a for a in (Z, Y, X) if a in order[phase + 1:]]
+        right, left, across = place.neighbour(axis, 1), place.neighbour(axis, -1), place.neighbour(axis, 2)
+
+        def chunk(by, half=None):
+            where = {**fixed, axis: place.shifted(axis, by)}
+            if half is not None:
+                where[free[0]] = pl.ds(2 * half, 2)
+            return full.at[at(where, ALL, cols)]
+
+        if not free:
+            src_by, half, peer, from_by = ((0, None, right, -1), (0, None, left, 1), (0, None, across, 2))[i]
+        else:
+            src_by, half, peer, from_by = ((0, None, right, -1), (0, None, left, 1), (-1, 0, right, 2), (1, 1, left, 2))[i]
+        out = chunk(src_by, half)
+        src = weight.at[:, cols] if not free else out
+        go = lambda: pltpu.make_async_remote_copy(src_ref=src, dst_ref=out, send_sem=ssem.at[part, phase, i], recv_sem=rsem.at[part, phase, i], device_id=peer, device_id_type=MESH)
+        came = chunk(from_by, half)
+        come = lambda: pltpu.make_async_remote_copy(src_ref=came, dst_ref=came, send_sem=ssem.at[part, phase, i], recv_sem=rsem.at[part, phase, i], device_id=peer, device_id_type=MESH)
+        return go, come
+
+    plan = {0: ((), (2, (0, 1, 2))), 1: ((2, (0, 1, 2)), (1, (0, 1))), 2: ((1, (0, 1)), (1, (2, 3))), 3: ((1, (2, 3)), (0, (0, 1))), 4: ((0, (0, 1)), (0, (2, 3))), 5: ((0, (2, 3)), ())}
+    waits, sends = plan[step]
+    if waits:
+        for i in waits[1]:
+            for part in range(3):
+                piece(part, waits[0], i)[1]().wait_recv()
+    if sends:
+        for i in sends[1]:
+            for part in range(3):
+                piece(part, sends[0], i)[0]().start()
+    if step == 5:
+        for phase, count in ((2, 3), (1, 4), (0, 4)):
+            for i in range(count):
+                for part in range(3):
+                    piece(part, phase, i)[0]().wait_send()
+
+
+def muon_kernel(grad, momentum, weight, new_momentum, new_weight, weight_bf16, mine, other, acc, half, xm, xo, gram, poly, part_gram, full, stage, *scratch):
     ring = scratch[:12]
-    load_sem, pair_ssem, pair_rsem, rs_ssem, rs_rsem, ag_ssem, ag_rsem, fw_ssem, fw_rsem = scratch[12:]
+    load_sem, pair_ssem, pair_rsem, rs_ssem, rs_rsem, ag_ssem, ag_rsem, fw_ssem, fw_rsem, wg_ssem, wg_rsem, xc_ssem, xc_rsem, out_sem, po_ssem, po_rsem = scratch[12:]
     place = Place()
+    z, y, x = place.xyz
     stages = (2, 1, -1, 0)
     loads, swaps = {}, {}
     for s, by in enumerate(stages):
         for p, (first, width, order) in enumerate(PARTS):
             axis = order[0]
-            block = {axis: place.shifted(axis, by)}
-            z, y, x, r, c = at(block, ALL, pl.ds(first, width))
-            loads[p, by] = pltpu.make_async_copy(grad.at[z, y, x, place.core, r, c], acc.at[z, y, x, r, c], load_sem.at[p, s])
+            bz, bly, bx, r, c = at({axis: place.shifted(axis, by)}, ALL, pl.ds(first, width))
+            loads[p, by] = pltpu.make_async_copy(grad.at[bz, bly, bx, place.core, r, c], acc.at[bz, bly, bx, r, c], load_sem.at[p, s])
             loads[p, by].start()
     greet(place)
     for s, by in enumerate(stages):
         for p, (first, width, order) in enumerate(PARTS):
             axis = order[0]
-            block = {axis: place.shifted(axis, by)}
-            z, y, x, r, c = at(block, ALL, pl.ds(first, width))
-            swaps[p, by] = send(grad.at[z, y, x, 1 - place.core, r, c], half.at[z, y, x, r, c], pair_ssem.at[p, s], pair_rsem.at[p, s], place.partner())
+            bz, bly, bx, r, c = at({axis: place.shifted(axis, by)}, ALL, pl.ds(first, width))
+            swaps[p, by] = send(grad.at[bz, bly, bx, 1 - place.core, r, c], half.at[bz, bly, bx, r, c], pair_ssem.at[p, s], pair_rsem.at[p, s], place.partner())
+    full[z, y, x] = weight[...]
+    wstep = lambda i: weight_step(place, weight, full, wg_ssem, wg_rsem, i)
+    wstep(0)
 
     def ready(part):
         def chunk_ready(by):
@@ -210,7 +264,6 @@
     for phase in range(3):
         sent += run_together([reduce_phase(place, acc, ring[4 * phase:4 * phase + 4], rs_ssem, rs_rsem, p, phase, ready(p) if phase == 0 else (lambda by: None)) for p in range(3)])
 
-    z, y, x = place.xyz
     g = acc[z, y, x] / GROUP
     mom = MOMENTUM * momentum[...] + g
     new_momentum[...] = mom
@@ -225,55 +278,118 @@
 
     for phase in (2, 1, 0):
         sent += run_together([gather_phase(place, mine, ag_ssem, ag_rsem, p, phase, forward(p) if phase == 0 else (lambda i, w: None)) for p in range(3)])
+    wstep(1)
     for copy in forwards:
         copy.wait_recv()
     for copy in sent + forwards:
         copy.wait_send()
 
-
-def comm(grad, momentum):
+    total = jnp.zeros((8, COLS), jnp.float32)
+    for buf in (mine, other):
+        for i in range(RING):
+            block = buf[i].reshape(BLK // 8, 8, COLS).astype(jnp.float32)
+            total += jnp.sum(block * block, axis=0)
+    norm = jnp.sqrt(jnp.sum(jnp.sum(total, axis=0, keepdims=True), axis=1, keepdims=True))
+    inverse = 1.0 / (norm + 1e-7)
+    for buf, dst in ((mine, xm), (other, xo)):
+        for i in range(RING):
+            block = (buf[i].reshape(BLK, COLS).astype(jnp.float32) * inverse).astype(jnp.bfloat16)
+            dst[0, :, i * BLK:(i + 1) * BLK] = block.T
+
+    def exchange(slot, n):
+        cols = pl.ds(n * BLK, BLK)
+        return pltpu.make_async_remote_copy(src_ref=xm.at[slot, :, cols], dst_ref=xo.at[slot, :, cols], send_sem=xc_ssem.at[slot, n], recv_sem=xc_rsem.at[slot, n], device_id=place.partner(), device_id_type=MESH)
+
+    def mirror(dst, j, tall):
+        dst[j * BLK:, j * BLK:(j + 1) * BLK] = tall
+        if j < NBLK - 1:
+            dst[j * BLK:(j + 1) * BLK, (j + 1) * BLK:] = tall[BLK:].T
+
+    def newton_schulz(t, carry):
+        now = lax.rem(t, 2)
+        before = 1 - now
+        for when, step in ((0, 2), (1, 3), (3, 4)):
+            @pl.when(t == when)
+            def _():
+                wstep(step)
+
+        @pl.when(t > 0)
+        def _():
+            for n in range(NBLK):
+                cols = slice(n * BLK, (n + 1) * BLK)
+                old = xm[before, :, cols]
+                xm[now, :, cols] = (COEF_A * old.astype(jnp.float32) + dot(poly[...], old)).astype(jnp.bfloat16)
+                exchange(now, n).start()
+
+        for j in range(NBLK):
+            rows = slice(j * BLK, COLS)
+            part_gram[rows, j * BLK:(j + 1) * BLK] = lax.dot_general(xm[now, rows], xm[now, j * BLK:(j + 1) * BLK], NT, preferred_element_type=jnp.float32)
+
+        @pl.when(t > 0)
+        def _():
+            for n in range(NBLK):
+                exchange(now, n).wait()
+
+        for j in range(NBLK):
+            rows, cols = slice(j * BLK, COLS), slice(j * BLK, (j + 1) * BLK)
+            tall = part_gram[rows, cols] + lax.dot_general(xo[now, rows], xo[now, cols], NT, preferred_element_type=jnp.float32)
+            mirror(gram, j, tall.astype(jnp.bfloat16))
+        for j in range(NBLK):
+            rows, cols = slice(j * BLK, COLS), slice(j * BLK, (j + 1) * BLK)
+            tall = COEF_B * gram[rows, cols].astype(jnp.float32) + COEF_C * dot(gram[rows, :], gram[:, cols])
+            mirror(poly, j, tall.astype(jnp.bfloat16))
+        return carry
+
+    lax.fori_loop(0, NS_STEPS, newton_schulz, 0)
+    wstep(5)
+    last = (NS_STEPS - 1) % 2
+    scale = 0.2 * math.sqrt(ROWS)
+    outs = []
+    for n in range(NBLK):
+        cols = slice(n * BLK, (n + 1) * BLK)
+        old = xm[last, :, cols]
+        ortho = (COEF_A * old.astype(jnp.float32) + dot(poly[...], old)).astype(jnp.bfloat16)
+        w = full[n]
+        w = w - LEARN_RATE * (scale * ortho.T.astype(jnp.float32).reshape(w.shape) + WEIGHT_DECAY * w)
+        full[n] = w
+        stage[n] = w.astype(jnp.bfloat16)
+        there = weight_bf16.at[n, :, :, place.core]
+        outs.append(pltpu.make_async_copy(stage.at[n], there, out_sem.at[n]))
+        outs[-1].start()
+        outs.append(send(stage.at[n], there, po_ssem.at[n], po_rsem.at[n], place.partner()))
+    new_weight[...] = full[z, y, x]
+    for copy in outs:
+        copy.wait()
+
+
+def muon(grad, momentum, weight):
     ring = []
     for lead in ((RING, RING), (RING,), ()):
         ring += [pltpu.VMEM(lead + (SLAB, COLS), jnp.float32)] * 2 + [pltpu.VMEM(lead + (8, COLS), jnp.float32)] * 2
     dma = pltpu.SemaphoreType.DMA
     cube = (RING, RING, RING, SLAB, COLS)
     vmem = pl.BlockSpec(memory_space=pltpu.VMEM)
+    anywhere = pl.BlockSpec(memory_space=pl.ANY)
+    f32, bf16 = jnp.float32, jnp.bfloat16
     return pl.pallas_call(
-        comm_kernel,
-        out_shape=(jax.ShapeDtypeStruct((SLAB, COLS), jnp.float32), jax.ShapeDtypeStruct(cube, jnp.bfloat16), jax.ShapeDtypeStruct(cube, jnp.bfloat16)),
-        in_specs=[pl.BlockSpec(memory_space=pl.ANY), vmem],
-        out_specs=(vmem, vmem, vmem),
-        scratch_shapes=[pltpu.VMEM(cube, jnp.float32), pltpu.VMEM(cube, jnp.float32), *ring,
-                        dma((3, 4)), dma((3, 4)), dma((3, 4)), dma((3, 3, 6)), dma((3, 3, 6)), dma((3, 3, 4)), dma((3, 3, 4)), dma((3, 5)), dma((3, 5))],
-        compiler_params=pltpu.CompilerParams(collective_id=0, has_side_effects=True, vmem_limit_bytes=60 << 20),
-        name='reduce_gather',
-    )(grad, momentum)
-
-
-def orthogonalise(update):
-    as_float = update.astype(jnp.float32)
-    sq_norm = jnp.sum(as_float * as_float)
-    ortho = (as_float / (jnp.sqrt(sq_norm) + 1e-7)).astype(jnp.bfloat16)
-    for _ in range(NS_STEPS):
-        gram = jnp.einsum('lk,lj->kj', ortho, ortho, preferred_element_type=jnp.float32).astype(jnp.bfloat16)
-        gram_sq = jnp.einsum('kj,ji->ki', gram, gram, preferred_element_type=jnp.float32)
-        poly = (COEF_B * gram.astype(jnp.float32) + COEF_C * gram_sq).astype(jnp.bfloat16)
-        ortho = (COEF_A * ortho.astype(jnp.float32) + jnp.einsum('kj,lj->lk', poly, ortho, preferred_element_type=jnp.float32)).astype(jnp.bfloat16)
-    return ortho
+        muon_kernel,
+        out_shape=(jax.ShapeDtypeStruct((SLAB, COLS), f32), jax.ShapeDtypeStruct((SLAB, COLS), f32), jax.ShapeDtypeStruct((RING, RING, RING, 2, SLAB, COLS), bf16)),
+        in_specs=[anywhere, vmem, vmem],
+        out_specs=(vmem, vmem, anywhere),
+        scratch_shapes=[pltpu.VMEM(cube, bf16), pltpu.VMEM(cube, bf16), pltpu.VMEM(cube, f32), pltpu.VMEM(cube, f32),
+                        pltpu.VMEM((2, COLS, COLS), bf16), pltpu.VMEM((2, COLS, COLS), bf16), pltpu.VMEM((COLS, COLS), bf16), pltpu.VMEM((COLS, COLS), bf16),
+                        pltpu.VMEM((COLS, COLS), f32), pltpu.VMEM(cube, f32), pltpu.VMEM(cube, bf16), *ring,
+                        dma((3, 4)), dma((3, 4)), dma((3, 4)), dma((3, 3, 6)), dma((3, 3, 6)), dma((3, 3, 4)), dma((3, 3, 4)), dma((3, 5)), dma((3, 5)),
+                        dma((3, 3, 4)), dma((3, 3, 4)), dma((2, NBLK)), dma((2, NBLK)), dma((NBLK,)), dma((NBLK,)), dma((NBLK,))],
+        compiler_params=pltpu.CompilerParams(collective_id=0, has_side_effects=True, vmem_limit_bytes=62 << 20),
+        name='muon',
+    )(grad, momentum, weight)
 
 
 def solution(mesh):
     def local_step(grad_part, momentum, weight):
         grad = grad_part.reshape(RING, RING, RING, 2, SLAB, COLS)
-        new_momentum, mine, other = comm(grad, momentum[0])
-        core = lax.rem(lax.axis_index('dp'), 2)
-        first = core == 0
-        pair = jnp.stack([jnp.where(first, mine, other), jnp.where(first, other, mine)], axis=3)
-        ortho = orthogonalise(pair.reshape(ROWS, COLS))
-        slab = lax.dynamic_slice(ortho, (lax.axis_index('dp') * SLAB, 0), (SLAB, COLS))
-        scale = 0.2 * math.sqrt(ROWS)
-        new_weight = weight - LEARN_RATE * (scale * slab.astype(jnp.float32)[None] + WEIGHT_DECAY * weight)
-        weight_bf16 = lax.all_gather(new_weight.astype(jnp.bfloat16), 'dp', axis=1, tiled=True)
-        return new_momentum[None], new_weight, weight_bf16
+        new_momentum, new_weight, weight_bf16 = muon(grad, momentum[0], weight[0])
+        return new_momentum[None], new_weight[None], weight_bf16.reshape(1, ROWS, COLS)
 
     return jax.shard_map(local_step, mesh=mesh, in_specs=(P(('mp', 'dp')), P('mp', 'dp'), P('mp', 'dp')), out_specs=(P('mp', 'dp'), P('mp', 'dp'), P('mp')), check_vma=False)

time: 263 us -> 128 us (0.49)
  matrix products: 96.7 us -> 0 us
  waiting for transfers between devices: 63.5 us -> 0 us
  Pallas kernels: 66.6 us -> 119 us
  between operations: 15.1 us -> 0.64 us
  other arithmetic: 9.55 us -> 0 us
    dot_general x10 -> x0, matrix products: 96.7 us -> none  [the longest x5 59.8 us: orthogonalise(): jnp.einsum('kj,lj->lk', poly, ortho, preferred_element_type=jnp.float32)]
    all_gather x1 -> x0, waiting for transfers between devices: 63.5 us -> none  [local_step(): lax.all_gather(new_weight.astype(jnp.bfloat16), 'dp', axis=1, tiled=True)]
    pallas_call x1, Pallas kernels: 66.6 us -> 119 us  [muon(): pl.pallas_call(muon_kernel, out_shape=(jax.ShapeDtypeStruct((SLAB, COLS),...]
    convert_element_type x2 -> x0, other arithmetic: 3.76 us -> none  [the longest x1 2.26 us: orthogonalise(): ortho = (as_float / (jnp.sqrt(sq_norm) + 1e-07)).astype(jnp.bfloat16)]
    reduce_sum x1 -> x0, other arithmetic: 3.28 us -> none  [orthogonalise(): sq_norm = jnp.sum(as_float * as_float)]
    unnamed x8 -> x3, local copies, waits for them, and re-layouts: 6.59 us -> 7.59 us
  transfers between devices with their start and end apart: 1 -> 0, of which waited for: 1 -> 0; matrix products, arithmetic and copies ran while one was open for 0% -> 0% of each run, Pallas kernels for 0% -> 0%
where the time goes in v2:
time: 128 us; the launch traced here: 127 us
  Pallas kernels  119 us (93%)
  local copies, waits for them, and re-layouts  7.59 us (6%)
    pallas_call x1, Pallas kernels, muon(): pl.pallas_call(muon_kernel, out_shape=(jax.ShapeDtypeStruct((SLAB, COLS),...  119 us
    unnamed x3, local copies, waits for them, and re-layouts  7.59 us

profile of v2, /device:TPU:1, one launch (start us, length us, event | category | flops | bytes accessed | tf_op | source)
XLA Modules:
  0.0 127.4 jit_solution(8890276722679817275)
XLA Ops:
  0.6 119.2 %muon.1 = (f32[16,1024]{1,0:T(8,128)}, f32[16,1024]{1,0:T(8,128)}, bf16[4,4,4,2,16,1024]{5,4,3,2,1,0:T(8,128)(2,1)}) custom-call(f32[4,4,4,2,16,1024]{5,4,3,2,1,0:T(8,128)} %bitcast.6, f32[16,1024]{1,0:T(8,128)} %bitcast.8, f32[16,1024]{1,0:T(8,128)} %bitcast.9), custom_call_target="tpu_custom_call" | custom-call | tf_op jit(solution)/shard_map/muon/pallas_call | solution.py:374
  119.8 1.5 %copy.9 = f32[1,16,1024]{2,1,0:T(8,128)} copy(f32[1,16,1024]{2,1,0:T(8,128)} %bitcast.11) | data formatting | bytes 131072
  121.3 1.5 %copy.10 = f32[1,16,1024]{2,1,0:T(8,128)} copy(f32[1,16,1024]{2,1,0:T(8,128)} %bitcast.10) | data formatting | bytes 131072
  122.8 4.6 %copy.11 = bf16[1,2048,1024]{2,1,0:T(8,128)(2,1)} copy(bf16[1,2048,1024]{2,1,0:T(8,128)(2,1)} %bitcast.7) | data formatting | bytes 8388608

commit v3 on v2

--- a/solution.py
+++ b/solution.py
@@ -80,11 +80,21 @@
     def chunk(by, rows):
         return at({**fixed, axis: place.shifted(axis, by)}, rows, cols)
 
+    across = place.neighbour(axis, 2)
+
     def sub(rows):
         return tuple(ALL for _ in range(2 - phase)) + (rows, cols)
 
     started = []
     sems = lambda i: (ssem.at[part, phase, i], rsem.at[part, phase, i])
+    if phase == 2:
+        for i, (by, dst, peer) in enumerate(((2, far_l, across), (1, near_l, right), (-1, near_r, left))):
+            started.append(send(acc.at[chunk(by, ALL)], dst.at[sub(ALL)], *sems(i), peer))
+            yield
+        for copy in started:
+            copy.wait_recv()
+        acc[chunk(0, ALL)] += near_l[sub(ALL)] + near_r[sub(ALL)] + far_l[sub(ALL)]
+        return started
     ready(2)
     started.append(send(acc.at[chunk(2, LOW)], far_l.at[sub(ALL)], *sems(0), right))
     started.append(send(acc.at[chunk(2, HIGH)], far_r.at[sub(ALL)], *sems(1), left))
@@ -131,34 +141,34 @@
         pltpu.make_async_remote_copy(src_ref=there, dst_ref=there, send_sem=ssem.at[part, phase, i], recv_sem=rsem.at[part, phase, i], device_id=right, device_id_type=MESH).wait_recv()
 
     started = []
-    mine = buf.at[chunk(0)]
-    started.append(send(mine, mine, *sems(0), right))
-    started.append(send(mine, mine, *sems(1), left))
     if not free:
-        started.append(send(mine, mine, *sems(2), across))
-        on_piece(0, chunk(0))
+        mine = buf.at[chunk(0)]
+        for i, peer in enumerate((across, right, left)):
+            started.append(send(mine, mine, *sems(i), peer))
         yield
-        recv(0, -1)
-        recv(1, 1)
-        recv(2, 2)
-    else:
-        on_piece(0, chunk(0))
+        recv(1, -1)
+        recv(2, 1)
+        recv(0, 2)
+        return started
+    for i, half, peer in ((0, 0, right), (1, 1, left), (2, 1, right), (3, 0, left)):
+        mine = buf.at[chunk(0, half)]
+        started.append(send(mine, mine, *sems(i), peer))
+    on_piece(0, chunk(0))
+    yield
+    recv(0, -1, 0)
+    there = buf.at[chunk(-1, 0)]
+    started.append(send(there, there, *sems(4), right))
+    on_piece(1, chunk(-1, 0))
+    yield
+    recv(1, 1, 1)
+    there = buf.at[chunk(1, 1)]
+    started.append(send(there, there, *sems(5), left))
+    on_piece(2, chunk(1, 1))
+    yield
+    for i, by, half in ((2, -1, 1), (3, 1, 0), (4, 2, 0), (5, 2, 1)):
+        recv(i, by, half)
+        on_piece(i + 1, chunk(by, half))
         yield
-        recv(0, -1)
-        there = buf.at[chunk(-1, 0)]
-        started.append(send(there, there, *sems(2), right))
-        on_piece(1, chunk(-1))
-        yield
-        recv(1, 1)
-        there = buf.at[chunk(1, 1)]
-        started.append(send(there, there, *sems(3), left))
-        on_piece(2, chunk(1))
-        yield
-        recv(2, 2, 0)
-        on_piece(3, chunk(2, 0))
-        yield
-        recv(3, 2, 1)
-        on_piece(4, chunk(2, 1))
     return started
 
 
@@ -179,6 +189,17 @@
 NT = (((1,), (1,)), ((), ()))
 BLK = 256
 NBLK = COLS // BLK
+
+
+WIDE = 512
+
+
+def dot_nt(a, b):
+    return lax.dot_general(a, b, NT, preferred_element_type=jnp.float32)
+
+
+def square(n):
+    return slice((n % 2) * WIDE, (n % 2 + 1) * WIDE), slice((n // 2) * WIDE, (n // 2 + 1) * WIDE)
 
 
 def dot(a, b):
@@ -228,9 +249,9 @@
                     piece(part, phase, i)[0]().wait_send()
 
 
-def muon_kernel(grad, momentum, weight, new_momentum, new_weight, weight_bf16, mine, other, acc, half, xm, xo, gram, poly, part_gram, full, stage, *scratch):
+def muon_kernel(grad, momentum, weight, new_momentum, new_weight, weight_bf16, mine, other, acc, half, xm, xo, gram, poly, part_gram, full, old_mom, old_weight, *scratch):
     ring = scratch[:12]
-    load_sem, pair_ssem, pair_rsem, rs_ssem, rs_rsem, ag_ssem, ag_rsem, fw_ssem, fw_rsem, wg_ssem, wg_rsem, xc_ssem, xc_rsem, out_sem, po_ssem, po_rsem = scratch[12:]
+    load_sem, pair_ssem, pair_rsem, rs_ssem, rs_rsem, ag_ssem, ag_rsem, fw_ssem, fw_rsem, wg_ssem, wg_rsem, xc_ssem, xc_rsem, po_ssem, po_rsem, in_sem = scratch[12:]
     place = Place()
     z, y, x = place.xyz
     stages = (2, 1, -1, 0)
@@ -241,14 +262,19 @@
             bz, bly, bx, r, c = at({axis: place.shifted(axis, by)}, ALL, pl.ds(first, width))
             loads[p, by] = pltpu.make_async_copy(grad.at[bz, bly, bx, place.core, r, c], acc.at[bz, bly, bx, r, c], load_sem.at[p, s])
             loads[p, by].start()
+    into = (pltpu.make_async_copy(momentum, old_mom, in_sem.at[0]), pltpu.make_async_copy(weight, old_weight, in_sem.at[1]))
+    for copy in into:
+        copy.start()
     greet(place)
     for s, by in enumerate(stages):
         for p, (first, width, order) in enumerate(PARTS):
             axis = order[0]
             bz, bly, bx, r, c = at({axis: place.shifted(axis, by)}, ALL, pl.ds(first, width))
             swaps[p, by] = send(grad.at[bz, bly, bx, 1 - place.core, r, c], half.at[bz, bly, bx, r, c], pair_ssem.at[p, s], pair_rsem.at[p, s], place.partner())
-    full[z, y, x] = weight[...]
-    wstep = lambda i: weight_step(place, weight, full, wg_ssem, wg_rsem, i)
+    for copy in into:
+        copy.wait()
+    full[z, y, x] = old_weight[...]
+    wstep = lambda i: weight_step(place, old_weight, full, wg_ssem, wg_rsem, i)
     wstep(0)
 
     def ready(part):
@@ -265,7 +291,7 @@
         sent += run_together([reduce_phase(place, acc, ring[4 * phase:4 * phase + 4], rs_ssem, rs_rsem, p, phase, ready(p) if phase == 0 else (lambda by: None)) for p in range(3)])
 
     g = acc[z, y, x] / GROUP
-    mom = MOMENTUM * momentum[...] + g
+    mom = MOMENTUM * old_mom[...] + g
     new_momentum[...] = mom
     mine[z, y, x] = (g + MOMENTUM * mom).astype(jnp.bfloat16)
 
@@ -297,8 +323,8 @@
             dst[0, :, i * BLK:(i + 1) * BLK] = block.T
 
     def exchange(slot, n):
-        cols = pl.ds(n * BLK, BLK)
-        return pltpu.make_async_remote_copy(src_ref=xm.at[slot, :, cols], dst_ref=xo.at[slot, :, cols], send_sem=xc_ssem.at[slot, n], recv_sem=xc_rsem.at[slot, n], device_id=place.partner(), device_id_type=MESH)
+        rows, cols = square(n)
+        return pltpu.make_async_remote_copy(src_ref=xm.at[slot, rows, cols], dst_ref=xo.at[slot, rows, cols], send_sem=xc_ssem.at[slot, n], recv_sem=xc_rsem.at[slot, n], device_id=place.partner(), device_id_type=MESH)
 
     def mirror(dst, j, tall):
         dst[j * BLK:, j * BLK:(j + 1) * BLK] = tall
@@ -315,28 +341,33 @@
 
         @pl.when(t > 0)
         def _():
-            for n in range(NBLK):
-                cols = slice(n * BLK, (n + 1) * BLK)
+            for n in range(4):
+                rows, cols = square(n)
                 old = xm[before, :, cols]
-                xm[now, :, cols] = (COEF_A * old.astype(jnp.float32) + dot(poly[...], old)).astype(jnp.bfloat16)
+                xm[now, rows, cols] = (COEF_A * xm[before, rows, cols].astype(jnp.float32) + dot(poly[rows, :], old)).astype(jnp.bfloat16)
                 exchange(now, n).start()
 
         for j in range(NBLK):
             rows = slice(j * BLK, COLS)
-            part_gram[rows, j * BLK:(j + 1) * BLK] = lax.dot_general(xm[now, rows], xm[now, j * BLK:(j + 1) * BLK], NT, preferred_element_type=jnp.float32)
-
-        @pl.when(t > 0)
-        def _():
-            for n in range(NBLK):
-                exchange(now, n).wait()
-
+            part_gram[rows, j * BLK:(j + 1) * BLK] = dot_nt(xm[now, rows], xm[now, j * BLK:(j + 1) * BLK])
+
+        for k in range(2):
+            @pl.when(t > 0)
+            def _():
+                for n in (2 * k, 2 * k + 1):
+                    exchange(now, n).wait()
+
+            deep = slice(k * WIDE, (k + 1) * WIDE)
+            for j in range(NBLK):
+                rows, cols = slice(j * BLK, COLS), slice(j * BLK, (j + 1) * BLK)
+                tall = part_gram[rows, cols] + dot_nt(xo[now, rows, deep], xo[now, cols, deep])
+                if k == 0:
+                    part_gram[rows, cols] = tall
+                else:
+                    mirror(gram, j, tall.astype(jnp.bfloat16))
         for j in range(NBLK):
             rows, cols = slice(j * BLK, COLS), slice(j * BLK, (j + 1) * BLK)
-            tall = part_gram[rows, cols] + lax.dot_general(xo[now, rows], xo[now, cols], NT, preferred_element_type=jnp.float32)
-            mirror(gram, j, tall.astype(jnp.bfloat16))
-        for j in range(NBLK):
-            rows, cols = slice(j * BLK, COLS), slice(j * BLK, (j + 1) * BLK)
-            tall = COEF_B * gram[rows, cols].astype(jnp.float32) + COEF_C * dot(gram[rows, :], gram[:, cols])
+            tall = COEF_B * gram[rows, cols].astype(jnp.float32) + COEF_C * dot_nt(gram[rows, :], gram[cols, :])
             mirror(poly, j, tall.astype(jnp.bfloat16))
         return carry
 
@@ -346,17 +377,17 @@
     scale = 0.2 * math.sqrt(ROWS)
     outs = []
     for n in range(NBLK):
-        cols = slice(n * BLK, (n + 1) * BLK)
-        old = xm[last, :, cols]
-        ortho = (COEF_A * old.astype(jnp.float32) + dot(poly[...], old)).astype(jnp.bfloat16)
+        if n % 2 == 0:
+            cols = slice(n * BLK, n * BLK + WIDE)
+            old = xm[last, :, cols]
+            wide = (COEF_A * old.astype(jnp.float32) + dot(poly[...], old)).astype(jnp.bfloat16)
+        ortho = wide[:, (n % 2) * BLK:(n % 2 + 1) * BLK]
         w = full[n]
         w = w - LEARN_RATE * (scale * ortho.T.astype(jnp.float32).reshape(w.shape) + WEIGHT_DECAY * w)
         full[n] = w
-        stage[n] = w.astype(jnp.bfloat16)
+        weight_bf16[n, :, :, place.core] = w.astype(jnp.bfloat16)
         there = weight_bf16.at[n, :, :, place.core]
-        outs.append(pltpu.make_async_copy(stage.at[n], there, out_sem.at[n]))
-        outs[-1].start()
-        outs.append(send(stage.at[n], there, po_ssem.at[n], po_rsem.at[n], place.partner()))
+        outs.append(send(there, there, po_ssem.at[n], po_rsem.at[n], place.partner()))
     new_weight[...] = full[z, y, x]
     for copy in outs:
         copy.wait()
@@ -365,31 +396,53 @@
 def muon(grad, momentum, weight):
     ring = []
     for lead in ((RING, RING), (RING,), ()):
-        ring += [pltpu.VMEM(lead + (SLAB, COLS), jnp.float32)] * 2 + [pltpu.VMEM(lead + (8, COLS), jnp.float32)] * 2
+        ring += [pltpu.VMEM(lead + (SLAB, COLS), jnp.float32)] * 2 + [pltpu.VMEM(lead + (8 if lead else SLAB, COLS), jnp.float32)] * 2
     dma = pltpu.SemaphoreType.DMA
     cube = (RING, RING, RING, SLAB, COLS)
     vmem = pl.BlockSpec(memory_space=pltpu.VMEM)
+    hbm = pl.BlockSpec(memory_space=pltpu.HBM)
     anywhere = pl.BlockSpec(memory_space=pl.ANY)
     f32, bf16 = jnp.float32, jnp.bfloat16
     return pl.pallas_call(
         muon_kernel,
         out_shape=(jax.ShapeDtypeStruct((SLAB, COLS), f32), jax.ShapeDtypeStruct((SLAB, COLS), f32), jax.ShapeDtypeStruct((RING, RING, RING, 2, SLAB, COLS), bf16)),
-        in_specs=[anywhere, vmem, vmem],
-        out_specs=(vmem, vmem, anywhere),
+        in_specs=[anywhere, hbm, hbm],
+        out_specs=(vmem, vmem, vmem),
         scratch_shapes=[pltpu.VMEM(cube, bf16), pltpu.VMEM(cube, bf16), pltpu.VMEM(cube, f32), pltpu.VMEM(cube, f32),
                         pltpu.VMEM((2, COLS, COLS), bf16), pltpu.VMEM((2, COLS, COLS), bf16), pltpu.VMEM((COLS, COLS), bf16), pltpu.VMEM((COLS, COLS), bf16),
-                        pltpu.VMEM((COLS, COLS), f32), pltpu.VMEM(cube, f32), pltpu.VMEM(cube, bf16), *ring,
-                        dma((3, 4)), dma((3, 4)), dma((3, 4)), dma((3, 3, 6)), dma((3, 3, 6)), dma((3, 3, 4)), dma((3, 3, 4)), dma((3, 5)), dma((3, 5)),
-                        dma((3, 3, 4)), dma((3, 3, 4)), dma((2, NBLK)), dma((2, NBLK)), dma((NBLK,)), dma((NBLK,)), dma((NBLK,))],
-        compiler_params=pltpu.CompilerParams(collective_id=0, has_side_effects=True, vmem_limit_bytes=62 << 20),
+                        pltpu.VMEM((COLS, COLS), f32), pltpu.VMEM(cube, f32), pltpu.VMEM((SLAB, COLS), f32), pltpu.VMEM((SLAB, COLS), f32), *ring,
+                        dma((3, 4)), dma((3, 4)), dma((3, 4)), dma((3, 3, 6)), dma((3, 3, 6)), dma((3, 3, 6)), dma((3, 3, 6)), dma((3, 7)), dma((3, 7)),
+                        dma((3, 3, 4)), dma((3, 3, 4)), dma((2, NBLK)), dma((2, NBLK)), dma((NBLK,)), dma((NBLK,)), dma((2,))],
+        compiler_params=pltpu.CompilerParams(collective_id=0, has_side_effects=True, vmem_limit_bytes=46 << 20),
         name='muon',
     )(grad, momentum, weight)
+
+
+def put_kernel(*refs):
+    sems = refs[-1]
+    copies = [pltpu.make_async_copy(refs[i], refs[3 + i], sems.at[i]) for i in (2, 1, 0)]
+    for copy in copies:
+        copy.start()
+    for copy in copies:
+        copy.wait()
+
+
+def put(*values):
+    return pl.pallas_call(
+        put_kernel,
+        out_shape=tuple(jax.ShapeDtypeStruct(v.shape, v.dtype) for v in values),
+        in_specs=[pl.BlockSpec(memory_space=pltpu.VMEM)] * 3,
+        out_specs=(pl.BlockSpec(memory_space=pltpu.HBM),) * 3,
+        scratch_shapes=[pltpu.SemaphoreType.DMA((3,))],
+        compiler_params=pltpu.CompilerParams(vmem_limit_bytes=8 << 20),
+        name='put',
+    )(*values)
 
 
 def solution(mesh):
     def local_step(grad_part, momentum, weight):
         grad = grad_part.reshape(RING, RING, RING, 2, SLAB, COLS)
-        new_momentum, new_weight, weight_bf16 = muon(grad, momentum[0], weight[0])
+        new_momentum, new_weight, weight_bf16 = put(*muon(grad, *(pltpu.with_memory_space_constraint(v[0], pltpu.HBM) for v in (momentum, weight))))
         return new_momentum[None], new_weight[None], weight_bf16.reshape(1, ROWS, COLS)
 
     return jax.shard_map(local_step, mesh=mesh, in_specs=(P(('mp', 'dp')), P('mp', 'dp'), P('mp', 'dp')), out_specs=(P('mp', 'dp'), P('mp', 'dp'), P('mp')), check_vma=False)

time: 128 us -> 109 us (0.85)
  Pallas kernels: 119 us -> 108 us
  local copies, waits for them, and re-layouts: 7.59 us -> 0 us
    pallas_call x1, Pallas kernels: 119 us -> 106 us  [muon(): pl.pallas_call(muon_kernel, out_shape=(jax.ShapeDtypeStruct((SLAB, COLS),...]
    unnamed x3 -> x0, local copies, waits for them, and re-layouts: 7.59 us -> none
    pallas_call x0 -> x1, Pallas kernels: none -> 2.06 us  [put(): pl.pallas_call(put_kernel, out_shape=tuple((jax.ShapeDtypeStruct(v.shape,...]
where the time goes in v3:
time: 109 us; the launch traced here: 108 us
  Pallas kernels  108 us (99%)
    pallas_call x1, Pallas kernels, muon(): pl.pallas_call(muon_kernel, out_shape=(jax.ShapeDtypeStruct((SLAB, COLS),...  106 us

profile of v3, /device:TPU:1, one launch (start us, length us, event | category | flops | bytes accessed | tf_op | source)
XLA Modules:
  0.0 108.5 jit_solution(6755705973295714305)
XLA Ops:
  0.6 105.6 %muon.1 = (f32[16,1024]{1,0:T(8,128)S(1)}, f32[16,1024]{1,0:T(8,128)S(1)}, bf16[4,4,4,2,16,1024]{5,4,3,2,1,0:T(8,128)(2,1)S(1)}) custom-call(f32[4,4,4,2,16,1024]{5,4,3,2,1,0:T(8,128)} %bitcast.6, f32[16,1024]{1,0:T(8,128)} %bitcast.7, f32[16,1024]{1,0:T(8,128)} %bitcast.8), custom_call_target="tpu_custom_call" | custom-call | tf_op jit(solution)/shard_map/muon/pallas_call | solution.py:406
  106.3 2.1 %put.1 = (f32[16,1024]{1,0:T(8,128)}, f32[16,1024]{1,0:T(8,128)}, bf16[4,4,4,2,16,1024]{5,4,3,2,1,0:T(8,128)(2,1)}) custom-call(f32[16,1024]{1,0:T(8,128)S(1)} %get-tuple-element.9.refs_0_, f32[16,1024]{1,0:T(8,128)S(1)} %get-tuple-element.10.refs_1_, bf16[4,4,4,2,16,1024]{5,4,3,2,1,0:T(8,128)(2,1)S(1)} %get-tuple-element.11.refs_2_), custom_call_target="tpu_custom_call" | custom-call | tf_op jit(solution)/shard_map/put/pallas_call | solution.py:431

commit v4 on v3

--- a/solution.py
+++ b/solution.py
@@ -66,124 +66,137 @@
 
 
 ALL = slice(None)
-LOW, HIGH = pl.ds(0, 8), pl.ds(8, 8)
-
-
-def reduce_phase(place, acc, ring_refs, ssem, rsem, part, phase, ready):
-    first, width, order = PARTS[part]
-    axis = order[phase]
-    cols = pl.ds(first, width)
-    near_l, near_r, far_l, far_r = ring_refs
-    fixed = {a: place.xyz[a] for a in order[:phase]}
-    right, left = place.neighbour(axis, 1), place.neighbour(axis, -1)
-
-    def chunk(by, rows):
-        return at({**fixed, axis: place.shifted(axis, by)}, rows, cols)
-
-    across = place.neighbour(axis, 2)
-
-    def sub(rows):
-        return tuple(ALL for _ in range(2 - phase)) + (rows, cols)
-
-    started = []
-    sems = lambda i: (ssem.at[part, phase, i], rsem.at[part, phase, i])
-    if phase == 2:
-        for i, (by, dst, peer) in enumerate(((2, far_l, across), (1, near_l, right), (-1, near_r, left))):
-            started.append(send(acc.at[chunk(by, ALL)], dst.at[sub(ALL)], *sems(i), peer))
-            yield
-        for copy in started:
+BATCHES = 1
+LEAD = SLAB // BATCHES
+STEPS = ('far0', 'near0', 'far1', 'near1', 'near2', 'all2', 'half1', 'full1', 'half0', 'rest0', 'full0')
+LAG = 0.5
+
+
+class Line:
+    def __init__(self, place, part, batch, phase):
+        first, width, order = PARTS[part]
+        self.place, self.axis = place, order[phase]
+        self.rows, self.cols = pl.ds(LEAD * batch, LEAD), pl.ds(first, width)
+        self.fixed = {a: place.xyz[a] for a in order[:phase]}
+        self.free = [a for a in (Z, Y, X) if a in order[phase + 1:]]
+        self.right, self.left, self.across = (place.neighbour(self.axis, by) for by in (1, -1, 2))
+
+    def chunk(self, by, half=None):
+        where = {**self.fixed, self.axis: self.place.shifted(self.axis, by)}
+        if half is not None:
+            where[self.free[0]] = pl.ds(2 * half, 2)
+        return at(where, self.rows, self.cols)
+
+    def slot(self, half=None):
+        lead = [ALL] * len(self.free)
+        if half is not None:
+            lead[0] = pl.ds(2 * half, 2)
+        return (*lead, self.rows, self.cols)
+
+
+def reduce_chain(place, acc, ring, ssem, rsem, part, batch, ready, sent):
+    for phase in range(3):
+        line = Line(place, part, batch, phase)
+        near_l, near_r, far_l, far_r = ring[4 * phase:4 * phase + 4]
+        chunk, slot, right, left = line.chunk, line.slot, line.right, line.left
+
+        def go(i, src, dst, peer):
+            copy = send(src, dst, ssem.at[part, batch, phase, i], rsem.at[part, batch, phase, i], peer)
+            sent.append(copy)
+            return copy
+
+        if phase == 2:
+            copies = [go(0, acc.at[chunk(2)], far_l.at[slot()], line.across), go(1, acc.at[chunk(1)], near_l.at[slot()], right), go(2, acc.at[chunk(-1)], near_r.at[slot()], left)]
+            yield 'near2'
+            for copy in copies:
+                copy.wait_recv()
+            acc[chunk(0)] += near_l[slot()] + near_r[slot()] + far_l[slot()]
+            continue
+        if phase == 0:
+            yield 'swap', 0
+            ready(2)
+        far = go(0, acc.at[chunk(2, 0)], far_l.at[slot()], right), go(1, acc.at[chunk(2, 1)], far_r.at[slot()], left)
+        if phase == 0:
+            yield 'swap', 1
+            ready(1)
+        near = [go(2, acc.at[chunk(1, 1)], near_l.at[slot(1)], right)]
+        if phase == 0:
+            yield 'swap', 2
+            ready(-1)
+        near.append(go(3, acc.at[chunk(-1, 0)], near_r.at[slot(0)], left))
+        if phase == 0:
+            yield 'swap', 3
+            ready(0)
+        yield 'far%d' % phase
+        far[0].wait_recv()
+        acc[chunk(1, 0)] += far_l[slot()]
+        near.append(go(4, acc.at[chunk(1, 0)], near_l.at[slot(0)], right))
+        yield 'far%d' % phase
+        far[1].wait_recv()
+        acc[chunk(-1, 1)] += far_r[slot()]
+        near.append(go(5, acc.at[chunk(-1, 1)], near_r.at[slot(1)], left))
+        yield 'near%d' % phase
+        for copy in near:
             copy.wait_recv()
-        acc[chunk(0, ALL)] += near_l[sub(ALL)] + near_r[sub(ALL)] + far_l[sub(ALL)]
-        return started
-    ready(2)
-    started.append(send(acc.at[chunk(2, LOW)], far_l.at[sub(ALL)], *sems(0), right))
-    started.append(send(acc.at[chunk(2, HIGH)], far_r.at[sub(ALL)], *sems(1), left))
-    yield
-    ready(1)
-    started.append(send(acc.at[chunk(1, HIGH)], near_l.at[sub(HIGH)], *sems(2), right))
-    yield
-    ready(-1)
-    started.append(send(acc.at[chunk(-1, LOW)], near_r.at[sub(LOW)], *sems(3), left))
-    yield
-    started[0].wait_recv()
-    acc[chunk(1, LOW)] += far_l[sub(ALL)]
-    started.append(send(acc.at[chunk(1, LOW)], near_l.at[sub(LOW)], *sems(4), right))
-    yield
-    started[1].wait_recv()
-    acc[chunk(-1, HIGH)] += far_r[sub(ALL)]
-    started.append(send(acc.at[chunk(-1, HIGH)], near_r.at[sub(HIGH)], *sems(5), left))
-    yield
-    ready(0)
-    yield
-    for i in (2, 3, 4, 5):
-        started[i].wait_recv()
-    acc[chunk(0, ALL)] += near_l[sub(ALL)] + near_r[sub(ALL)]
-    return started
-
-
-def gather_phase(place, buf, ssem, rsem, part, phase, on_piece):
-    first, width, order = PARTS[part]
-    axis = order[phase]
-    cols = pl.ds(first, width)
-    fixed = {a: place.xyz[a] for a in order[:phase]}
-    right, left, across = place.neighbour(axis, 1), place.neighbour(axis, -1), place.neighbour(axis, 2)
-    free = [a for a in (Z, Y, X) if a in order[phase + 1:]]
-    sems = lambda i: (ssem.at[part, phase, i], rsem.at[part, phase, i])
-
-    def chunk(by, half=None):
-        where = {**fixed, axis: place.shifted(axis, by)}
-        if half is not None:
-            where[free[0]] = pl.ds(2 * half, 2)
-        return at(where, ALL, cols)
-
-    def recv(i, by, half=None):
-        there = buf.at[chunk(by, half)]
-        pltpu.make_async_remote_copy(src_ref=there, dst_ref=there, send_sem=ssem.at[part, phase, i], recv_sem=rsem.at[part, phase, i], device_id=right, device_id_type=MESH).wait_recv()
-
-    started = []
-    if not free:
-        mine = buf.at[chunk(0)]
-        for i, peer in enumerate((across, right, left)):
-            started.append(send(mine, mine, *sems(i), peer))
-        yield
-        recv(1, -1)
-        recv(2, 1)
-        recv(0, 2)
-        return started
-    for i, half, peer in ((0, 0, right), (1, 1, left), (2, 1, right), (3, 0, left)):
-        mine = buf.at[chunk(0, half)]
-        started.append(send(mine, mine, *sems(i), peer))
-    on_piece(0, chunk(0))
-    yield
-    recv(0, -1, 0)
-    there = buf.at[chunk(-1, 0)]
-    started.append(send(there, there, *sems(4), right))
-    on_piece(1, chunk(-1, 0))
-    yield
-    recv(1, 1, 1)
-    there = buf.at[chunk(1, 1)]
-    started.append(send(there, there, *sems(5), left))
-    on_piece(2, chunk(1, 1))
-    yield
-    for i, by, half in ((2, -1, 1), (3, 1, 0), (4, 2, 0), (5, 2, 1)):
-        recv(i, by, half)
-        on_piece(i + 1, chunk(by, half))
-        yield
-    return started
-
-
-def run_together(generators):
-    started, live = [], list(generators)
-    while live:
-        left = []
-        for g in live:
-            try:
-                next(g)
-                left.append(g)
-            except StopIteration as stop:
-                started.extend(stop.value)
-        live = left
-    return started
+        acc[chunk(0)] += near_l[slot()] + near_r[slot()]
+
+
+def gather_chain(place, buf, ssem, rsem, part, batch, on_piece, sent):
+    for phase in (2, 1, 0):
+        line = Line(place, part, batch, phase)
+        chunk, right, left = line.chunk, line.right, line.left
+
+        def go(i, where, peer):
+            sent.append(send(buf.at[where], buf.at[where], ssem.at[part, batch, phase, i], rsem.at[part, batch, phase, i], peer))
+
+        def recv(i, where):
+            there = buf.at[where]
+            pltpu.make_async_remote_copy(src_ref=there, dst_ref=there, send_sem=ssem.at[part, batch, phase, i], recv_sem=rsem.at[part, batch, phase, i], device_id=right, device_id_type=MESH).wait_recv()
+
+        def piece(i, where):
+            if phase == 0:
+                on_piece(i, where)
+
+        if phase == 2:
+            for i, peer in enumerate((line.across, right, left)):
+                go(i, chunk(0), peer)
+            yield 'all2'
+            recv(1, chunk(-1))
+            recv(2, chunk(1))
+            recv(0, chunk(2))
+            continue
+        for i, half, peer in ((0, 0, right), (1, 1, left), (2, 1, right), (3, 0, left)):
+            go(i, chunk(0, half), peer)
+        piece(0, chunk(0))
+        yield 'half%d' % phase
+        recv(0, chunk(-1, 0))
+        go(4, chunk(-1, 0), right)
+        piece(1, chunk(-1, 0))
+        yield 'half%d' % phase
+        recv(1, chunk(1, 1))
+        go(5, chunk(1, 1), left)
+        piece(2, chunk(1, 1))
+        for i, by, half in ((2, -1, 1), (3, 1, 0), (4, 2, 0), (5, 2, 1)):
+            if i == 2 or i == 4:
+                yield 'full%d' % phase if i == 4 or phase == 1 else 'rest0'
+            recv(i, chunk(by, half))
+            piece(i + 1, chunk(by, half))
+
+
+def run_chains(chains):
+    queue = []
+
+    def step(number, batch, chain):
+        name = next(chain, None)
+        if name is not None:
+            due = batch - 9 + name[1] / 9 if isinstance(name, tuple) else STEPS.index(name) + LAG * batch
+            queue.append((due, number, batch, chain))
+
+    for number, (batch, chain) in enumerate(chains):
+        step(number, batch, chain)
+    while queue:
+        queue.sort(key=lambda entry: entry[:2])
+        step(*queue.pop(0)[1:])
 
 
 NT = (((1,), (1,)), ((), ()))
@@ -255,66 +268,64 @@
     place = Place()
     z, y, x = place.xyz
     stages = (2, 1, -1, 0)
-    loads, swaps = {}, {}
-    for s, by in enumerate(stages):
-        for p, (first, width, order) in enumerate(PARTS):
-            axis = order[0]
-            bz, bly, bx, r, c = at({axis: place.shifted(axis, by)}, ALL, pl.ds(first, width))
-            loads[p, by] = pltpu.make_async_copy(grad.at[bz, bly, bx, place.core, r, c], acc.at[bz, bly, bx, r, c], load_sem.at[p, s])
-            loads[p, by].start()
+    order = [(b, s, p) for b in range(BATCHES) for s in range(4) for p in range(3)]
+    loads, swaps, sent, forwards = {}, {}, [], []
+
+    def block(b, s, p):
+        axis = PARTS[p][2][0]
+        return at({axis: place.shifted(axis, stages[s])}, pl.ds(LEAD * b, LEAD), pl.ds(*PARTS[p][:2]))
+
+    for b, s, p in order:
+        bz, by, bx, r, c = here = block(b, s, p)
+        loads[p, b, stages[s]] = pltpu.make_async_copy(grad.at[bz, by, bx, place.core, r, c], acc.at[here], load_sem.at[p, b, s])
+        loads[p, b, stages[s]].start()
     into = (pltpu.make_async_copy(momentum, old_mom, in_sem.at[0]), pltpu.make_async_copy(weight, old_weight, in_sem.at[1]))
     for copy in into:
         copy.start()
     greet(place)
-    for s, by in enumerate(stages):
-        for p, (first, width, order) in enumerate(PARTS):
-            axis = order[0]
-            bz, bly, bx, r, c = at({axis: place.shifted(axis, by)}, ALL, pl.ds(first, width))
-            swaps[p, by] = send(grad.at[bz, bly, bx, 1 - place.core, r, c], half.at[bz, bly, bx, r, c], pair_ssem.at[p, s], pair_rsem.at[p, s], place.partner())
+    for b, s, p in order:
+        bz, by, bx, r, c = here = block(b, s, p)
+        swaps[p, b, stages[s]] = send(grad.at[bz, by, bx, 1 - place.core, r, c], half.at[here], pair_ssem.at[p, b, s], pair_rsem.at[p, b, s], place.partner())
     for copy in into:
         copy.wait()
     full[z, y, x] = old_weight[...]
     wstep = lambda i: weight_step(place, old_weight, full, wg_ssem, wg_rsem, i)
     wstep(0)
 
-    def ready(part):
-        def chunk_ready(by):
-            first, width, order = PARTS[part]
-            here = at({order[0]: place.shifted(order[0], by)}, ALL, pl.ds(first, width))
-            loads[part, by].wait()
-            swaps[part, by].wait_recv()
+    def chain(p, b):
+        cols, rows = pl.ds(*PARTS[p][:2]), pl.ds(LEAD * b, LEAD)
+
+        def ready(by):
+            here = block(b, stages.index(by), p)
+            loads[p, b, by].wait()
+            swaps[p, b, by].wait_recv()
             acc[here] += half[here]
-        return chunk_ready
-
-    sent = list(swaps.values())
-    for phase in range(3):
-        sent += run_together([reduce_phase(place, acc, ring[4 * phase:4 * phase + 4], rs_ssem, rs_rsem, p, phase, ready(p) if phase == 0 else (lambda by: None)) for p in range(3)])
-
-    g = acc[z, y, x] / GROUP
-    mom = MOMENTUM * old_mom[...] + g
-    new_momentum[...] = mom
-    mine[z, y, x] = (g + MOMENTUM * mom).astype(jnp.bfloat16)
-
-    forwards = []
-
-    def forward(part):
-        def on_piece(i, where):
-            forwards.append(send(mine.at[where], other.at[where], fw_ssem.at[part, i], fw_rsem.at[part, i], place.partner()))
-        return on_piece
-
-    for phase in (2, 1, 0):
-        sent += run_together([gather_phase(place, mine, ag_ssem, ag_rsem, p, phase, forward(p) if phase == 0 else (lambda i, w: None)) for p in range(3)])
+
+        def forward(i, where):
+            forwards.append(send(mine.at[where], other.at[where], fw_ssem.at[p, b, i], fw_rsem.at[p, b, i], place.partner()))
+
+        yield from reduce_chain(place, acc, ring, rs_ssem, rs_rsem, p, b, ready, sent)
+        g = acc[z, y, x, rows, cols] / GROUP
+        mom = MOMENTUM * old_mom[rows, cols] + g
+        new_momentum[rows, cols] = mom
+        mine[z, y, x, rows, cols] = (g + MOMENTUM * mom).astype(jnp.bfloat16)
+        yield from gather_chain(place, mine, ag_ssem, ag_rsem, p, b, forward, sent)
+
+    run_chains([(b, chain(p, b)) for b in range(BATCHES) for p in range(3)])
     wstep(1)
-    for copy in forwards:
-        copy.wait_recv()
-    for copy in sent + forwards:
-        copy.wait_send()
-
-    total = jnp.zeros((8, COLS), jnp.float32)
-    for buf in (mine, other):
+
+    def squares(buf, total):
         for i in range(RING):
             block = buf[i].reshape(BLK // 8, 8, COLS).astype(jnp.float32)
             total += jnp.sum(block * block, axis=0)
+        return total
+
+    total = squares(mine, jnp.zeros((8, COLS), jnp.float32))
+    for copy in forwards:
+        copy.wait_recv()
+    total = squares(other, total)
+    for copy in sent + forwards + list(swaps.values()):
+        copy.wait_send()
     norm = jnp.sqrt(jnp.sum(jnp.sum(total, axis=0, keepdims=True), axis=1, keepdims=True))
     inverse = 1.0 / (norm + 1e-7)
     for buf, dst in ((mine, xm), (other, xo)):
@@ -334,18 +345,14 @@
     def newton_schulz(t, carry):
         now = lax.rem(t, 2)
         before = 1 - now
-        for when, step in ((0, 2), (1, 3), (3, 4)):
-            @pl.when(t == when)
-            def _():
-                wstep(step)
-
         @pl.when(t > 0)
         def _():
-            for n in range(4):
-                rows, cols = square(n)
+            for k in range(2):
+                cols = slice(k * WIDE, (k + 1) * WIDE)
                 old = xm[before, :, cols]
-                xm[now, rows, cols] = (COEF_A * xm[before, rows, cols].astype(jnp.float32) + dot(poly[rows, :], old)).astype(jnp.bfloat16)
-                exchange(now, n).start()
+                xm[now, :, cols] = (COEF_A * old.astype(jnp.float32) + dot(poly[...], old)).astype(jnp.bfloat16)
+                exchange(now, 2 * k).start()
+                exchange(now, 2 * k + 1).start()
 
         for j in range(NBLK):
             rows = slice(j * BLK, COLS)
@@ -369,10 +376,14 @@
             rows, cols = slice(j * BLK, COLS), slice(j * BLK, (j + 1) * BLK)
             tall = COEF_B * gram[rows, cols].astype(jnp.float32) + COEF_C * dot_nt(gram[rows, :], gram[cols, :])
             mirror(poly, j, tall.astype(jnp.bfloat16))
+
+        for when, step in ((0, 2), (1, 3), (3, 4)):
+            @pl.when(t == when)
+            def _():
+                wstep(step)
         return carry
 
     lax.fori_loop(0, NS_STEPS, newton_schulz, 0)
-    wstep(5)
     last = (NS_STEPS - 1) % 2
     scale = 0.2 * math.sqrt(ROWS)
     outs = []
@@ -380,8 +391,10 @@
         if n % 2 == 0:
             cols = slice(n * BLK, n * BLK + WIDE)
             old = xm[last, :, cols]
-            wide = (COEF_A * old.astype(jnp.float32) + dot(poly[...], old)).astype(jnp.bfloat16)
-        ortho = wide[:, (n % 2) * BLK:(n % 2 + 1) * BLK]
+            pair = (COEF_A * old.astype(jnp.float32) + dot(poly[...], old)).astype(jnp.bfloat16)
+        if n == 0:
+            wstep(5)
+        ortho = pair[:, (n % 2) * BLK:(n % 2 + 1) * BLK]
         w = full[n]
         w = w - LEARN_RATE * (scale * ortho.T.astype(jnp.float32).reshape(w.shape) + WEIGHT_DECAY * w)
         full[n] = w
@@ -395,8 +408,8 @@
 
 def muon(grad, momentum, weight):
     ring = []
-    for lead in ((RING, RING), (RING,), ()):
-        ring += [pltpu.VMEM(lead + (SLAB, COLS), jnp.float32)] * 2 + [pltpu.VMEM(lead + (8 if lead else SLAB, COLS), jnp.float32)] * 2
+    for lead, split in (((RING, RING), (2, RING)), ((RING,), (2,)), ((), ())):
+        ring += [pltpu.VMEM(lead + (SLAB, COLS), jnp.float32)] * 2 + [pltpu.VMEM(split + (SLAB, COLS), jnp.float32)] * 2
     dma = pltpu.SemaphoreType.DMA
     cube = (RING, RING, RING, SLAB, COLS)
     vmem = pl.BlockSpec(memory_space=pltpu.VMEM)
@@ -411,7 +424,7 @@
         scratch_shapes=[pltpu.VMEM(cube, bf16), pltpu.VMEM(cube, bf16), pltpu.VMEM(cube, f32), pltpu.VMEM(cube, f32),
                         pltpu.VMEM((2, COLS, COLS), bf16), pltpu.VMEM((2, COLS, COLS), bf16), pltpu.VMEM((COLS, COLS), bf16), pltpu.VMEM((COLS, COLS), bf16),
                         pltpu.VMEM((COLS, COLS), f32), pltpu.VMEM(cube, f32), pltpu.VMEM((SLAB, COLS), f32), pltpu.VMEM((SLAB, COLS), f32), *ring,
-                        dma((3, 4)), dma((3, 4)), dma((3, 4)), dma((3, 3, 6)), dma((3, 3, 6)), dma((3, 3, 6)), dma((3, 3, 6)), dma((3, 7)), dma((3, 7)),
+                        *[dma((3, BATCHES, 4))] * 3, *[dma((3, BATCHES, 3, 6))] * 4, *[dma((3, BATCHES, 7))] * 2,
                         dma((3, 3, 4)), dma((3, 3, 4)), dma((2, NBLK)), dma((2, NBLK)), dma((NBLK,)), dma((NBLK,)), dma((2,))],
         compiler_params=pltpu.CompilerParams(collective_id=0, has_side_effects=True, vmem_limit_bytes=46 << 20),
         name='muon',

time: 109 us -> 106 us (0.972)
  Pallas kernels: 108 us -> 106 us
    pallas_call x1, Pallas kernels: 106 us -> 103 us  [muon(): pl.pallas_call(muon_kernel, out_shape=(jax.ShapeDtypeStruct((SLAB, COLS),...]
where the time goes in v4:
time: 106 us
  Pallas kernels  106 us (100%)
    pallas_call x1, Pallas kernels, muon(): pl.pallas_call(muon_kernel, out_shape=(jax.ShapeDtypeStruct((SLAB, COLS),...  103 us

profile of v4, /device:TPU:1, one launch (start us, length us, event | category | flops | bytes accessed | tf_op | source)
XLA Modules:
  0.0 106.3 jit_solution(1318519649540573930)
XLA Ops:
  0.6 103.5 %muon.1 = (f32[16,1024]{1,0:T(8,128)S(1)}, f32[16,1024]{1,0:T(8,128)S(1)}, bf16[4,4,4,2,16,1024]{5,4,3,2,1,0:T(8,128)(2,1)S(1)}) custom-call(f32[4,4,4,2,16,1024]{5,4,3,2,1,0:T(8,128)} %bitcast.6, f32[16,1024]{1,0:T(8,128)} %bitcast.7, f32[16,1024]{1,0:T(8,128)} %bitcast.8), custom_call_target="tpu_custom_call" | custom-call | tf_op jit(solution)/shard_map/muon/pallas_call | solution.py:419
  104.1 2.1 %put.1 = (f32[16,1024]{1,0:T(8,128)}, f32[16,1024]{1,0:T(8,128)}, bf16[4,4,4,2,16,1024]{5,4,3,2,1,0:T(8,128)(2,1)}) custom-call(f32[16,1024]{1,0:T(8,128)S(1)} %get-tuple-element.9.refs_0_, f32[16,1024]{1,0:T(8,128)S(1)} %get-tuple-element.10.refs_1_, bf16[4,4,4,2,16,1024]{5,4,3,2,1,0:T(8,128)(2,1)S(1)} %get-tuple-element.11.refs_2_), custom_call_target="tpu_custom_call" | custom-call | tf_op jit(solution)/shard_map/put/pallas_call | solution.py:444

commit v5 on v4

--- a/solution.py
+++ b/solution.py
@@ -66,137 +66,195 @@
 
 
 ALL = slice(None)
-BATCHES = 1
-LEAD = SLAB // BATCHES
-STEPS = ('far0', 'near0', 'far1', 'near1', 'near2', 'all2', 'half1', 'full1', 'half0', 'rest0', 'full0')
-LAG = 0.5
+TURNS = (2, 1, -1, 0)
 
 
 class Line:
-    def __init__(self, place, part, batch, phase):
+    def __init__(self, place, part, phase):
         first, width, order = PARTS[part]
-        self.place, self.axis = place, order[phase]
-        self.rows, self.cols = pl.ds(LEAD * batch, LEAD), pl.ds(first, width)
+        self.place, self.axis, self.cols = place, order[phase], pl.ds(first, width)
         self.fixed = {a: place.xyz[a] for a in order[:phase]}
         self.free = [a for a in (Z, Y, X) if a in order[phase + 1:]]
+        self.next, self.last = (order[1] if phase == 0 else None), order[2]
         self.right, self.left, self.across = (place.neighbour(self.axis, by) for by in (1, -1, 2))
 
-    def chunk(self, by, half=None):
-        where = {**self.fixed, self.axis: self.place.shifted(self.axis, by)}
+    def narrowed(self, turn, half):
+        where = {}
+        if turn is not None:
+            where[self.next] = self.place.shifted(self.next, turn)
         if half is not None:
-            where[self.free[0]] = pl.ds(2 * half, 2)
-        return at(where, self.rows, self.cols)
-
-    def slot(self, half=None):
-        lead = [ALL] * len(self.free)
-        if half is not None:
-            lead[0] = pl.ds(2 * half, 2)
-        return (*lead, self.rows, self.cols)
-
-
-def reduce_chain(place, acc, ring, ssem, rsem, part, batch, ready, sent):
-    for phase in range(3):
-        line = Line(place, part, batch, phase)
-        near_l, near_r, far_l, far_r = ring[4 * phase:4 * phase + 4]
-        chunk, slot, right, left = line.chunk, line.slot, line.right, line.left
-
-        def go(i, src, dst, peer):
-            copy = send(src, dst, ssem.at[part, batch, phase, i], rsem.at[part, batch, phase, i], peer)
-            sent.append(copy)
-            return copy
-
-        if phase == 2:
-            copies = [go(0, acc.at[chunk(2)], far_l.at[slot()], line.across), go(1, acc.at[chunk(1)], near_l.at[slot()], right), go(2, acc.at[chunk(-1)], near_r.at[slot()], left)]
-            yield 'near2'
-            for copy in copies:
-                copy.wait_recv()
-            acc[chunk(0)] += near_l[slot()] + near_r[slot()] + far_l[slot()]
-            continue
-        if phase == 0:
-            yield 'swap', 0
-            ready(2)
-        far = go(0, acc.at[chunk(2, 0)], far_l.at[slot()], right), go(1, acc.at[chunk(2, 1)], far_r.at[slot()], left)
-        if phase == 0:
-            yield 'swap', 1
-            ready(1)
-        near = [go(2, acc.at[chunk(1, 1)], near_l.at[slot(1)], right)]
-        if phase == 0:
-            yield 'swap', 2
-            ready(-1)
-        near.append(go(3, acc.at[chunk(-1, 0)], near_r.at[slot(0)], left))
-        if phase == 0:
-            yield 'swap', 3
-            ready(0)
-        yield 'far%d' % phase
+            where[self.last] = pl.ds(2 * half, 2)
+        return where
+
+    def chunk(self, by, half=None, turn=None):
+        return at({**self.fixed, self.axis: self.place.shifted(self.axis, by), **self.narrowed(turn, half)}, ALL, self.cols)
+
+    def slot(self, half=None, turn=None):
+        where = self.narrowed(turn, half)
+        return (*(where.get(a, ALL) for a in self.free), ALL, self.cols)
+
+
+def chain_steps(place, acc, ring, rs_ssem, rs_rsem, buf, ag_ssem, ag_rsem, part, ready, update, on_piece, sent):
+    outer, middle, inner = (Line(place, part, phase) for phase in range(3))
+
+    def start(bufs, sems, peer, *index):
+        copy = send(*bufs, sems[0].at[(part, *index)], sems[1].at[(part, *index)], peer)
+        sent.append(copy)
+        return copy
+
+    def reduce_send(line, phase, turn, i, where, slot, dst, peer):
+        return start((acc.at[where], dst.at[slot]), (rs_ssem, rs_rsem), peer, phase + (turn or 0), i)
+
+    def far_and_own(line, refs, k, turn, ready):
+        near_l, near_r, far_l, far_r = refs
+        ready(2)
+        far = (reduce_send(line, k, 0, 0, line.chunk(2, 0, turn), line.slot(0, turn), far_l, line.right), reduce_send(line, k, 0, 1, line.chunk(2, 1, turn), line.slot(1, turn), far_r, line.left))
+        ready(1)
+        near = [reduce_send(line, k, 0, 2, line.chunk(1, 1, turn), line.slot(1, turn), near_l, line.right)]
+        ready(-1)
+        near.append(reduce_send(line, k, 0, 3, line.chunk(-1, 0, turn), line.slot(0, turn), near_r, line.left))
+        ready(0)
+        return far, near
+
+    def combine(line, refs, k, turn, far, near):
+        near_l, near_r, far_l, far_r = refs
         far[0].wait_recv()
-        acc[chunk(1, 0)] += far_l[slot()]
-        near.append(go(4, acc.at[chunk(1, 0)], near_l.at[slot(0)], right))
-        yield 'far%d' % phase
+        acc[line.chunk(1, 0, turn)] += far_l[line.slot(0, turn)]
+        near.append(reduce_send(line, k, 0, 4, line.chunk(1, 0, turn), line.slot(0, turn), near_l, line.right))
         far[1].wait_recv()
-        acc[chunk(-1, 1)] += far_r[slot()]
-        near.append(go(5, acc.at[chunk(-1, 1)], near_r.at[slot(1)], left))
-        yield 'near%d' % phase
+        acc[line.chunk(-1, 1, turn)] += far_r[line.slot(1, turn)]
+        near.append(reduce_send(line, k, 0, 5, line.chunk(-1, 1, turn), line.slot(1, turn), near_r, line.left))
+
+    def settle(line, refs, turn, near):
         for copy in near:
             copy.wait_recv()
-        acc[chunk(0)] += near_l[slot()] + near_r[slot()]
-
-
-def gather_chain(place, buf, ssem, rsem, part, batch, on_piece, sent):
-    for phase in (2, 1, 0):
-        line = Line(place, part, batch, phase)
-        chunk, right, left = line.chunk, line.right, line.left
-
-        def go(i, where, peer):
-            sent.append(send(buf.at[where], buf.at[where], ssem.at[part, batch, phase, i], rsem.at[part, batch, phase, i], peer))
-
-        def recv(i, where):
-            there = buf.at[where]
-            pltpu.make_async_remote_copy(src_ref=there, dst_ref=there, send_sem=ssem.at[part, batch, phase, i], recv_sem=rsem.at[part, batch, phase, i], device_id=right, device_id_type=MESH).wait_recv()
-
-        def piece(i, where):
-            if phase == 0:
-                on_piece(i, where)
-
-        if phase == 2:
-            for i, peer in enumerate((line.across, right, left)):
-                go(i, chunk(0), peer)
-            yield 'all2'
-            recv(1, chunk(-1))
-            recv(2, chunk(1))
-            recv(0, chunk(2))
-            continue
-        for i, half, peer in ((0, 0, right), (1, 1, left), (2, 1, right), (3, 0, left)):
-            go(i, chunk(0, half), peer)
-        piece(0, chunk(0))
-        yield 'half%d' % phase
-        recv(0, chunk(-1, 0))
-        go(4, chunk(-1, 0), right)
-        piece(1, chunk(-1, 0))
-        yield 'half%d' % phase
-        recv(1, chunk(1, 1))
-        go(5, chunk(1, 1), left)
-        piece(2, chunk(1, 1))
-        for i, by, half in ((2, -1, 1), (3, 1, 0), (4, 2, 0), (5, 2, 1)):
-            if i == 2 or i == 4:
-                yield 'full%d' % phase if i == 4 or phase == 1 else 'rest0'
-            recv(i, chunk(by, half))
-            piece(i + 1, chunk(by, half))
+        acc[line.chunk(0, None, turn)] += refs[0][line.slot(None, turn)] + refs[1][line.slot(None, turn)]
+
+    first, second, third = ring[0:4], ring[4:8], ring[8:12]
+    state = {}
+
+    def open_turn(k):
+        state[k] = far_and_own(outer, first, k, TURNS[k], lambda by: ready(by, k))
+
+    def close_turn(k):
+        combine(outer, first, k, TURNS[k], *state[k])
+
+    def end_turn(k):
+        settle(outer, first, TURNS[k], state[k][1])
+
+    middle_near = []
+
+    def middle_send(i, by, half, dst, peer):
+        return reduce_send(middle, 4, 0, i, middle.chunk(by, half), middle.slot(half), dst, peer)
+
+    open_turn(0)
+    yield
+    open_turn(1)
+    yield
+    close_turn(0)
+    yield
+    open_turn(2)
+    yield
+    close_turn(1)
+    yield
+    open_turn(3)
+    yield
+    close_turn(2)
+    yield
+    end_turn(0)
+    middle_far = (middle_send(0, 2, 0, second[2], middle.right), middle_send(1, 2, 1, second[3], middle.left))
+    yield
+    close_turn(3)
+    yield
+    end_turn(1)
+    middle_near.append(middle_send(2, 1, 1, second[0], middle.right))
+    yield
+    end_turn(2)
+    middle_near.append(middle_send(3, -1, 0, second[1], middle.left))
+    yield
+    combine(middle, second, 4, None, middle_far, middle_near)
+    yield
+    end_turn(3)
+    yield
+    settle(middle, second, None, middle_near)
+    near_l, near_r, far_l, _ = third
+    slot = inner.slot()
+    copies = [reduce_send(inner, 5, 0, i, inner.chunk(by), slot, dst, peer) for i, by, dst, peer in ((0, 2, far_l, inner.across), (1, 1, near_l, inner.right), (2, -1, near_r, inner.left))]
+    yield
+    for copy in copies:
+        copy.wait_recv()
+    acc[inner.chunk(0)] += near_l[slot] + near_r[slot] + far_l[slot]
+    update()
+
+    def go(k, i, where, peer):
+        start((buf.at[where], buf.at[where]), (ag_ssem, ag_rsem), peer, k, i)
+
+    def recv(k, i, where):
+        there = buf.at[where]
+        pltpu.make_async_remote_copy(src_ref=there, dst_ref=there, send_sem=ag_ssem.at[part, k, i], recv_sem=ag_rsem.at[part, k, i], device_id=inner.right, device_id_type=MESH).wait_recv()
+
+    def spread(k):
+        where = outer.chunk(0, None, TURNS[k])
+        go(k, 0, where, outer.right)
+        go(k, 1, where, outer.left)
+        on_piece(k, 0, where)
+
+    def pass_on(k):
+        turn = TURNS[k]
+        recv(k, 0, outer.chunk(-1, None, turn))
+        go(k, 2, outer.chunk(-1, 0, turn), outer.right)
+        on_piece(k, 1, outer.chunk(-1, None, turn))
+        recv(k, 1, outer.chunk(1, None, turn))
+        go(k, 3, outer.chunk(1, 1, turn), outer.left)
+        on_piece(k, 2, outer.chunk(1, None, turn))
+
+    def take(k):
+        for half in (0, 1):
+            where = outer.chunk(2, half, TURNS[k])
+            recv(k, 2 + half, where)
+            on_piece(k, 3 + half, where)
+
+    for i, peer in enumerate((inner.across, inner.right, inner.left)):
+        go(5, i, inner.chunk(0), peer)
+    yield
+    for i, by in ((1, -1), (2, 1), (0, 2)):
+        recv(5, i, inner.chunk(by))
+    for i, half, peer in ((0, 0, middle.right), (1, 1, middle.left), (2, 1, middle.right), (3, 0, middle.left)):
+        go(4, i, middle.chunk(0, half), peer)
+    spread(3)
+    yield
+    recv(4, 0, middle.chunk(-1, 0))
+    go(4, 4, middle.chunk(-1, 0), middle.right)
+    recv(4, 1, middle.chunk(1, 1))
+    go(4, 5, middle.chunk(1, 1), middle.left)
+    yield
+    recv(4, 2, middle.chunk(-1, 1))
+    spread(2)
+    recv(4, 3, middle.chunk(1, 0))
+    spread(1)
+    yield
+    pass_on(3)
+    yield
+    recv(4, 4, middle.chunk(2, 0))
+    recv(4, 5, middle.chunk(2, 1))
+    spread(0)
+    yield
+    pass_on(2)
+    pass_on(1)
+    yield
+    take(3)
+    yield
+    pass_on(0)
+    yield
+    take(2)
+    take(1)
+    yield
+    take(0)
 
 
 def run_chains(chains):
-    queue = []
-
-    def step(number, batch, chain):
-        name = next(chain, None)
-        if name is not None:
-            due = batch - 9 + name[1] / 9 if isinstance(name, tuple) else STEPS.index(name) + LAG * batch
-            queue.append((due, number, batch, chain))
-
-    for number, (batch, chain) in enumerate(chains):
-        step(number, batch, chain)
-    while queue:
-        queue.sort(key=lambda entry: entry[:2])
-        step(*queue.pop(0)[1:])
+    while chains:
+        chains = [chain for chain in chains if next(chain, chain) is not chain]
 
 
 NT = (((1,), (1,)), ((), ()))
@@ -267,51 +325,51 @@
     load_sem, pair_ssem, pair_rsem, rs_ssem, rs_rsem, ag_ssem, ag_rsem, fw_ssem, fw_rsem, wg_ssem, wg_rsem, xc_ssem, xc_rsem, po_ssem, po_rsem, in_sem = scratch[12:]
     place = Place()
     z, y, x = place.xyz
-    stages = (2, 1, -1, 0)
-    order = [(b, s, p) for b in range(BATCHES) for s in range(4) for p in range(3)]
+    order = [(k, by, p) for k in range(4) for by in TURNS for p in range(3)]
     loads, swaps, sent, forwards = {}, {}, [], []
 
-    def block(b, s, p):
-        axis = PARTS[p][2][0]
-        return at({axis: place.shifted(axis, stages[s])}, pl.ds(LEAD * b, LEAD), pl.ds(*PARTS[p][:2]))
-
-    for b, s, p in order:
-        bz, by, bx, r, c = here = block(b, s, p)
-        loads[p, b, stages[s]] = pltpu.make_async_copy(grad.at[bz, by, bx, place.core, r, c], acc.at[here], load_sem.at[p, b, s])
-        loads[p, b, stages[s]].start()
+    def block(k, by, p):
+        first, width, (outer, middle, _) = PARTS[p]
+        return at({outer: place.shifted(outer, by), middle: place.shifted(middle, TURNS[k])}, ALL, pl.ds(first, width))
+
+    for k, by, p in order:
+        bz, bly, bx, r, c = here = block(k, by, p)
+        loads[p, k, by] = pltpu.make_async_copy(grad.at[bz, bly, bx, place.core, r, c], acc.at[here], load_sem.at[p, k, TURNS.index(by)])
+        loads[p, k, by].start()
     into = (pltpu.make_async_copy(momentum, old_mom, in_sem.at[0]), pltpu.make_async_copy(weight, old_weight, in_sem.at[1]))
     for copy in into:
         copy.start()
     greet(place)
-    for b, s, p in order:
-        bz, by, bx, r, c = here = block(b, s, p)
-        swaps[p, b, stages[s]] = send(grad.at[bz, by, bx, 1 - place.core, r, c], half.at[here], pair_ssem.at[p, b, s], pair_rsem.at[p, b, s], place.partner())
+    for k, by, p in order:
+        bz, bly, bx, r, c = here = block(k, by, p)
+        swaps[p, k, by] = send(grad.at[bz, bly, bx, 1 - place.core, r, c], half.at[here], pair_ssem.at[p, k, TURNS.index(by)], pair_rsem.at[p, k, TURNS.index(by)], place.partner())
     for copy in into:
         copy.wait()
     full[z, y, x] = old_weight[...]
     wstep = lambda i: weight_step(place, old_weight, full, wg_ssem, wg_rsem, i)
     wstep(0)
 
-    def chain(p, b):
-        cols, rows = pl.ds(*PARTS[p][:2]), pl.ds(LEAD * b, LEAD)
-
-        def ready(by):
-            here = block(b, stages.index(by), p)
-            loads[p, b, by].wait()
-            swaps[p, b, by].wait_recv()
+    def chain(p):
+        cols = pl.ds(*PARTS[p][:2])
+
+        def ready(by, k):
+            here = block(k, by, p)
+            loads[p, k, by].wait()
+            swaps[p, k, by].wait_recv()
             acc[here] += half[here]
 
-        def forward(i, where):
-            forwards.append(send(mine.at[where], other.at[where], fw_ssem.at[p, b, i], fw_rsem.at[p, b, i], place.partner()))
-
-        yield from reduce_chain(place, acc, ring, rs_ssem, rs_rsem, p, b, ready, sent)
-        g = acc[z, y, x, rows, cols] / GROUP
-        mom = MOMENTUM * old_mom[rows, cols] + g
-        new_momentum[rows, cols] = mom
-        mine[z, y, x, rows, cols] = (g + MOMENTUM * mom).astype(jnp.bfloat16)
-        yield from gather_chain(place, mine, ag_ssem, ag_rsem, p, b, forward, sent)
-
-    run_chains([(b, chain(p, b)) for b in range(BATCHES) for p in range(3)])
+        def update():
+            g = acc[z, y, x, :, cols] / GROUP
+            mom = MOMENTUM * old_mom[:, cols] + g
+            new_momentum[:, cols] = mom
+            mine[z, y, x, :, cols] = (g + MOMENTUM * mom).astype(jnp.bfloat16)
+
+        def forward(k, i, where):
+            forwards.append(send(mine.at[where], other.at[where], fw_ssem.at[p, k, i], fw_rsem.at[p, k, i], place.partner()))
+
+        return chain_steps(place, acc, ring, rs_ssem, rs_rsem, mine, ag_ssem, ag_rsem, p, ready, update, forward, sent)
+
+    run_chains([chain(p) for p in range(3)])
     wstep(1)
 
     def squares(buf, total):
@@ -408,8 +466,8 @@
 
 def muon(grad, momentum, weight):
     ring = []
-    for lead, split in (((RING, RING), (2, RING)), ((RING,), (2,)), ((), ())):
-        ring += [pltpu.VMEM(lead + (SLAB, COLS), jnp.float32)] * 2 + [pltpu.VMEM(split + (SLAB, COLS), jnp.float32)] * 2
+    for lead in ((RING, RING), (RING,), ()):
+        ring += [pltpu.VMEM(lead + (SLAB, COLS), jnp.float32)] * 4
     dma = pltpu.SemaphoreType.DMA
     cube = (RING, RING, RING, SLAB, COLS)
     vmem = pl.BlockSpec(memory_space=pltpu.VMEM)
@@ -424,7 +482,7 @@
         scratch_shapes=[pltpu.VMEM(cube, bf16), pltpu.VMEM(cube, bf16), pltpu.VMEM(cube, f32), pltpu.VMEM(cube, f32),
                         pltpu.VMEM((2, COLS, COLS), bf16), pltpu.VMEM((2, COLS, COLS), bf16), pltpu.VMEM((COLS, COLS), bf16), pltpu.VMEM((COLS, COLS), bf16),
                         pltpu.VMEM((COLS, COLS), f32), pltpu.VMEM(cube, f32), pltpu.VMEM((SLAB, COLS), f32), pltpu.VMEM((SLAB, COLS), f32), *ring,
-                        *[dma((3, BATCHES, 4))] * 3, *[dma((3, BATCHES, 3, 6))] * 4, *[dma((3, BATCHES, 7))] * 2,
+                        *[dma((3, 4, 4))] * 3, *[dma((3, 6, 6))] * 4, *[dma((3, 4, 5))] * 2,
                         dma((3, 3, 4)), dma((3, 3, 4)), dma((2, NBLK)), dma((2, NBLK)), dma((NBLK,)), dma((NBLK,)), dma((2,))],
         compiler_params=pltpu.CompilerParams(collective_id=0, has_side_effects=True, vmem_limit_bytes=46 << 20),
         name='muon',

time: 106 us -> 106 us (level)
  no operation moved by 1% of the time
where the time goes in v5:
time: 106 us
  Pallas kernels  105 us (99%)
    pallas_call x1, Pallas kernels, muon(): pl.pallas_call(muon_kernel, out_shape=(jax.ShapeDtypeStruct((SLAB, COLS),...  103 us

profile of v5, /device:TPU:1, one launch (start us, length us, event | category | flops | bytes accessed | tf_op | source)
XLA Modules:
  0.0 105.7 jit_solution(3529882104622782979)
XLA Ops:
  0.6 102.9 %muon.1 = (f32[16,1024]{1,0:T(8,128)S(1)}, f32[16,1024]{1,0:T(8,128)S(1)}, bf16[4,4,4,2,16,1024]{5,4,3,2,1,0:T(8,128)(2,1)S(1)}) custom-call(f32[4,4,4,2,16,1024]{5,4,3,2,1,0:T(8,128)} %bitcast.6, f32[16,1024]{1,0:T(8,128)} %bitcast.7, f32[16,1024]{1,0:T(8,128)} %bitcast.8), custom_call_target="tpu_custom_call" | custom-call | tf_op jit(solution)/shard_map/muon/pallas_call | solution.py:477
  103.5 2.1 %put.1 = (f32[16,1024]{1,0:T(8,128)}, f32[16,1024]{1,0:T(8,128)}, bf16[4,4,4,2,16,1024]{5,4,3,2,1,0:T(8,128)(2,1)}) custom-call(f32[16,1024]{1,0:T(8,128)S(1)} %get-tuple-element.9.refs_0_, f32[16,1024]{1,0:T(8,128)S(1)} %get-tuple-element.10.refs_1_, bf16[4,4,4,2,16,1024]{5,4,3,2,1,0:T(8,128)(2,1)S(1)} %get-tuple-element.11.refs_2_), custom_call_target="tpu_custom_call" | custom-call | tf_op jit(solution)/shard_map/put/pallas_call | solution.py:502

commit v6 on v5

--- a/solution.py
+++ b/solution.py
@@ -229,11 +229,11 @@
     go(4, 5, middle.chunk(1, 1), middle.left)
     yield
     recv(4, 2, middle.chunk(-1, 1))
+    recv(4, 3, middle.chunk(1, 0))
+    yield
+    pass_on(3)
     spread(2)
-    recv(4, 3, middle.chunk(1, 0))
     spread(1)
-    yield
-    pass_on(3)
     yield
     recv(4, 4, middle.chunk(2, 0))
     recv(4, 5, middle.chunk(2, 1))
@@ -252,9 +252,13 @@
     take(0)
 
 
-def run_chains(chains):
+def run_chains(chains, after_first):
+    first = True
     while chains:
         chains = [chain for chain in chains if next(chain, chain) is not chain]
+        if first:
+            after_first()
+        first = False
 
 
 NT = (((1,), (1,)), ((), ()))
@@ -343,11 +347,13 @@
     for k, by, p in order:
         bz, bly, bx, r, c = here = block(k, by, p)
         swaps[p, k, by] = send(grad.at[bz, bly, bx, 1 - place.core, r, c], half.at[here], pair_ssem.at[p, k, TURNS.index(by)], pair_rsem.at[p, k, TURNS.index(by)], place.partner())
-    for copy in into:
-        copy.wait()
-    full[z, y, x] = old_weight[...]
     wstep = lambda i: weight_step(place, old_weight, full, wg_ssem, wg_rsem, i)
-    wstep(0)
+
+    def first_turn_out():
+        for copy in into:
+            copy.wait()
+        full[z, y, x] = old_weight[...]
+        wstep(0)
 
     def chain(p):
         cols = pl.ds(*PARTS[p][:2])
@@ -369,7 +375,7 @@
 
         return chain_steps(place, acc, ring, rs_ssem, rs_rsem, mine, ag_ssem, ag_rsem, p, ready, update, forward, sent)
 
-    run_chains([chain(p) for p in range(3)])
+    run_chains([chain(p) for p in range(3)], first_turn_out)
     wstep(1)
 
     def squares(buf, total):

time: 106 us -> 106 us (level)
  no operation moved by 1% of the time
where the time goes in v6:
time: 106 us
  Pallas kernels  106 us (100%)
    pallas_call x1, Pallas kernels, muon(): pl.pallas_call(muon_kernel, out_shape=(jax.ShapeDtypeStruct((SLAB, COLS),...  103 us

profile of v6, /device:TPU:1, one launch (start us, length us, event | category | flops | bytes accessed | tf_op | source)
XLA Modules:
  0.0 106.3 jit_solution(13272843133665454053)
XLA Ops:
  0.6 103.4 %muon.1 = (f32[16,1024]{1,0:T(8,128)S(1)}, f32[16,1024]{1,0:T(8,128)S(1)}, bf16[4,4,4,2,16,1024]{5,4,3,2,1,0:T(8,128)(2,1)S(1)}) custom-call(f32[4,4,4,2,16,1024]{5,4,3,2,1,0:T(8,128)} %bitcast.6, f32[16,1024]{1,0:T(8,128)} %bitcast.7, f32[16,1024]{1,0:T(8,128)} %bitcast.8), custom_call_target="tpu_custom_call" | custom-call | tf_op jit(solution)/shard_map/muon/pallas_call | solution.py:483
  104.1 2.1 %put.1 = (f32[16,1024]{1,0:T(8,128)}, f32[16,1024]{1,0:T(8,128)}, bf16[4,4,4,2,16,1024]{5,4,3,2,1,0:T(8,128)(2,1)}) custom-call(f32[16,1024]{1,0:T(8,128)S(1)} %get-tuple-element.9.refs_0_, f32[16,1024]{1,0:T(8,128)S(1)} %get-tuple-element.10.refs_1_, bf16[4,4,4,2,16,1024]{5,4,3,2,1,0:T(8,128)(2,1)S(1)} %get-tuple-element.11.refs_2_), custom_call_target="tpu_custom_call" | custom-call | tf_op jit(solution)/shard_map/put/pallas_call | solution.py:508
